TPU v7x, 32 devices: a 4x4x1 block of a 4x4x8 slice. The times are simulated.
32 devices in a mesh: dp: 1 (over z), sp: 32 (over y, x, core).
Axes of the slice: x: 4, y: 4, z: 1, core: 2. Of those that a mesh axis runs over, the one named last changes fastest.
The devices are a block of a 4x4x8 slice.
Arguments:
- resid: float32 [8, 2048, 2048], P('dp', 'sp')
- pre_norm: float32 [2, 2048], replicated
- w_in: bfloat16 [2, 2048, 8512], replicated
- conv_w: float32 [2, 4352, 4], replicated
- conv_b: float32 [2, 4352], replicated
- dt_bias: float32 [2, 64], replicated
- a_log: float32 [2, 64], replicated
- d_skip: float32 [2, 64], replicated
- gate_norm: float32 [2, 1, 4096], replicated
- w_out: bfloat16 [2, 4096, 2048], replicated
Outputs:
- output 1: float32 [8, 2048, 2048], P('dp', 'sp')
- output 2: float32 [8, 2, 64, 64, 128], P('dp', None, 'sp')
- output 3: bfloat16 [8, 2, 4352, 3], P('dp')
All inputs are finite; a program needn't handle non-finite values.
Results may differ from a plain program's by a relative error of at most 0.0188396.
Values are sent between devices in bfloat16 or wider.
A program may use at most 768 MiB of HBM per device.

v0:
```python
import jax
import jax.numpy as jnp
from jax import lax
from jax.sharding import PartitionSpec as P

CONV_WIDTH = 4
CHUNK = 256
EPSILON = 1e-5


def rms_norm(values, gain_vec):
    mean_sq = jnp.mean(values * values, axis=-1, keepdims=True)
    return values * lax.rsqrt(mean_sq + EPSILON) * gain_vec


def ssd_scan(x_in, dt_in, bc_in, a_neg, d_vec):
    batch, seq_len, groups, per_group, head_dim = x_in.shape
    d_state = bc_in.shape[-1]
    causal = jnp.arange(CHUNK)[:, None] >= jnp.arange(CHUNK)[None, :]

    def body(chunk_index, carry):
        state, y_buffer = carry
        start = chunk_index * CHUNK
        x_chunk = lax.dynamic_slice_in_dim(x_in, start, CHUNK, axis=1)
        dt_chunk = lax.dynamic_slice_in_dim(dt_in, start, CHUNK, axis=1).astype(jnp.float32)
        bc_chunk = lax.dynamic_slice_in_dim(bc_in, start, CHUNK, axis=1)
        b_chunk = bc_chunk[:, :, 0]
        c_chunk = bc_chunk[:, :, 1]
        cum_log = jnp.cumsum(dt_chunk * a_neg, axis=1)
        cum_heads = jnp.transpose(cum_log, (0, 2, 3, 1))
        log_diff = cum_heads[..., :, None] - cum_heads[..., None, :]
        decay_mat = jnp.exp(jnp.where(causal, log_diff, -jnp.inf))
        scores = jnp.einsum('btgn,bsgn->bgts', c_chunk, b_chunk, preferred_element_type=jnp.float32)
        mix_mat = decay_mat * scores[:, :, None]
        x_float = x_chunk.astype(jnp.float32)
        x_scaled = x_float * dt_chunk[..., None]
        y_intra = jnp.einsum('bghts,bsghp->btghp', mix_mat, x_scaled, preferred_element_type=jnp.float32)
        y_inter = jnp.einsum('btgn,bghpn->btghp', c_chunk.astype(jnp.float32), state, preferred_element_type=jnp.float32)
        to_end = jnp.exp(cum_log[:, -1:] - cum_log)
        state = state * jnp.exp(cum_log[:, -1])[..., None, None] + jnp.einsum('bsghp,bsgn->bghpn', x_scaled * to_end[..., None], b_chunk.astype(jnp.float32), preferred_element_type=jnp.float32)
        y_chunk = y_intra + y_inter * jnp.exp(cum_log)[..., None] + d_vec[:, :, None] * x_float
        y_buffer = lax.dynamic_update_slice_in_dim(y_buffer, y_chunk.astype(jnp.bfloat16), start, axis=1)
        return state, y_buffer

    state_zero = jnp.zeros((batch, groups, per_group, head_dim, d_state), jnp.float32)
    y_zero = jnp.zeros(x_in.shape, jnp.bfloat16)
    return lax.fori_loop(0, seq_len // CHUNK, body, (state_zero, y_zero))


def solution(mesh):
    seg_count = mesh.shape['sp']

    def layer(resid, pre_w, w_in_l, conv_w_l, conv_b_l, dt_b, a_log_l, d_l, gate_w, w_out_l):
        batch, seg_len, d_model = resid.shape
        n_groups, group_width = gate_w.shape
        d_inner = n_groups * group_width
        n_heads = dt_b.shape[0]
        conv_dim = conv_b_l.shape[0]
        d_state = (conv_dim - d_inner) // (2 * n_groups)
        head_dim = d_inner // n_heads
        seq_len = seg_len * seg_count
        local_heads = n_heads // seg_count
        local_groups = max(n_groups // seg_count, 1)
        local_per_group = local_heads // local_groups
        repeat_count = max(seg_count // n_groups, 1)
        seg_index = lax.axis_index('sp')

        normed = rms_norm(resid, pre_w).astype(jnp.bfloat16)
        projected = jnp.einsum('bld,de->ble', normed, w_in_l, preferred_element_type=jnp.float32).astype(jnp.bfloat16)
        gate_z = projected[..., :d_inner]
        xbc = projected[..., d_inner:d_inner + conv_dim]
        dt_raw = projected[..., d_inner + conv_dim:]
        halo_rows = lax.ppermute(xbc[:, seg_len - (CONV_WIDTH - 1):], 'sp', [(source, source + 1) for source in range(seg_count - 1)])
        padded = jnp.concatenate([halo_rows, xbc], axis=1)
        conv_out = conv_b_l + sum(padded[:, tap_index:tap_index + seg_len].astype(jnp.float32) * conv_w_l[:, tap_index] for tap_index in range(CONV_WIDTH))
        activated = jax.nn.silu(conv_out).astype(jnp.bfloat16)
        delta = jax.nn.softplus(dt_raw.astype(jnp.float32) + dt_b).astype(jnp.bfloat16)
        bc_tokens = jnp.repeat(activated[..., d_inner:].reshape(batch, seg_len, 2, n_groups, d_state), repeat_count, axis=3)

        x_local = lax.all_to_all(activated[..., :d_inner], 'sp', 2, 1, tiled=True)
        dt_local = lax.all_to_all(delta, 'sp', 2, 1, tiled=True)
        bc_local = lax.all_to_all(bc_tokens, 'sp', 3, 1, tiled=True)

        head_start = seg_index * local_heads
        a_neg = -jnp.exp(lax.dynamic_slice_in_dim(a_log_l, head_start, local_heads)).reshape(local_groups, local_per_group)
        d_local = lax.dynamic_slice_in_dim(d_l, head_start, local_heads).reshape(local_groups, local_per_group)
        final, y_local = ssd_scan(x_local.reshape(batch, seq_len, local_groups, local_per_group, head_dim), dt_local.reshape(batch, seq_len, local_groups, local_per_group), bc_local, a_neg, d_local)

        y_tokens = lax.all_to_all(y_local.reshape(batch, seq_len, local_heads * head_dim), 'sp', 1, 2, tiled=True)

        gated = y_tokens.reshape(batch, seg_len, n_groups, group_width).astype(jnp.float32) * jax.nn.silu(gate_z.reshape(batch, seg_len, n_groups, group_width).astype(jnp.float32))
        normed_y = (gated * lax.rsqrt(jnp.mean(gated * gated, axis=-1, keepdims=True) + EPSILON) * gate_w).astype(jnp.bfloat16)
        out_proj = jnp.einsum('blgc,gcd->bld', normed_y, w_out_l.reshape(n_groups, group_width, d_model), preferred_element_type=jnp.float32)
        tail_rows = jnp.where(seg_index == seg_count - 1, xbc[:, seg_len - (CONV_WIDTH - 1):], jnp.zeros((), jnp.bfloat16))
        conv_state = lax.psum(tail_rows, 'sp')
        return resid + out_proj, final.reshape(batch, local_heads, head_dim, d_state), jnp.swapaxes(conv_state, 1, 2)

    def forward(resid, pre_norm, w_in, conv_w, conv_b, dt_bias, a_log, d_skip, gate_norm, w_out):
        finals = []
        tails = []
        for layer_index in range(w_in.shape[0]):
            resid, final, tail_rows = layer(resid, pre_norm[layer_index], w_in[layer_index], conv_w[layer_index], conv_b[layer_index], dt_bias[layer_index], a_log[layer_index], d_skip[layer_index], gate_norm[layer_index], w_out[layer_index])
            finals.append(final)
            tails.append(tail_rows)
        return resid, jnp.stack(finals, axis=1), jnp.stack(tails, axis=1)

    return jax.shard_map(forward, mesh=mesh, in_specs=(P('dp', 'sp', None), P(), P(), P(), P(), P(), P(), P(), P(), P()), out_specs=(P('dp', 'sp', None), P('dp', None, 'sp', None, None), P('dp', None, None, None)), check_vma=False)
```

profile of v0, /device:TPU:97, one launch (start us, length us, event | category | flops | bytes accessed | tf_op | source)
XLA Modules:
  0.0 988.4 jit_solution(16848445811704025407)
XLA Ops:
  11.1 26.6 %fusion.114 = bf16[8,64,8512]{2,1,0:T(8,128)(2,1)} fusion(bf16[2,2048,8512]{1,2,0:T(8,128)(2,1)} %param.16, f32[8,64,2048]{2,1,0:T(8,128)} %param.14, f32[2048]{0:T(1024)S(1)} %bitcast.437, f32[8,64]{1,0:T(8,128)S(1)} %add_rsqrt_fusion.3), kind=kOutput, calls=%fused_computation.132 | convolution fusion | flops 17858461696 | bytes 47785984 | tf_op jit(solution)/shard_map/bld,de->ble/dot_general | solution.py:69
  39.8 4.6 collective-permute-start
  46.9 7.5 all-to-all-start
  56.7 7.1 multiply_convert_fusion.1
  65.8 2.6 slice.271
  68.4 10.0 %copy.177 = bf16[8,64,4096]{1,0,2:T(8,128)(2,1)} copy(bf16[8,64,4096]{2,1,0:T(8,128)(2,1)} %slice.271) | data formatting | bytes 8388608 | tf_op jit(solution)/shard_map/slice | solution.py:80
  78.4 13.9 %reshape.594 = bf16[32,2,32768]{2,1,0:T(2,128)(2,1)} reshape(bf16[4096,8,64]{2,1,0:T(8,128)(2,1)} %bitcast.404) | data formatting | bytes 8388608
  92.3 6.3 all-to-all-start.1
  99.6 49.5 %all-to-all-done.1 = bf16[32,2,32768]{2,1,0:T(2,128)(2,1)} async-done(((bf16[32,2,32768]{2,1,0:T(2,128)(2,1)}), bf16[32,2,32768]{2,1,0:T(2,128)(2,1)}, u32[]{:S(2)}, u32[]{:S(2)}) %all-to-all-start.1) | async-done | bytes 4194336 | tf_op jit(solution)/shard_map/all_to_all | solution.py:80
  149.1 5.4 reshape.535
  154.5 7.9 all-to-all-start.2
  164.0 13.7 %reshape.595 = bf16[4096,8,64]{2,1,0:T(8,128)(2,1)} reshape(bf16[32,2,32768]{2,1,0:T(2,128)(2,1)} %all-to-all-done.1) | data formatting | bytes 8388608
  177.7 12.0 %copy.251 = bf16[8,64,32,128]{1,2,3,0:T(8,128)(2,1)} copy(bf16[8,64,32,128]{1,0,3,2:T(8,128)(2,1)} %bitcast.406) | data formatting | bytes 8388608 | tf_op jit(solution)/shard_map/all_to_all | solution.py:80
  189.8 12.3 %reshape.533 = bf16[8,2048,1,2,64]{1,4,3,0,2:T(8,128)(2,1)} reshape(bf16[8,32,64,128]{2,1,3,0:T(8,128)(2,1)} %bitcast.407) | data formatting | bytes 8388608 | tf_op jit(solution)/shard_map/reshape | solution.py:87
  202.1 58.5 %all-to-all-done.2 = bf16[8,64,2,32,128]{4,1,0,2,3:T(8,128)(2,1)} async-done(((bf16[8,64,2,32,128]{4,1,0,2,3:T(8,128)(2,1)}), bf16[8,64,2,32,128]{4,1,0,2,3:T(8,128)(2,1)}, u32[]{:S(2)}, u32[]{:S(2)}) %all-to-all-start.2) | async-done | bytes 8388640 | tf_op jit(solution)/shard_map/all_to_all | solution.py:82
  260.6 9.6 copy.180
  270.2 2.5 broadcast.177.clone
  272.7 82.4 %while.32 = (s32[]{:T(128)}, f32[8,1,2,64,128]{4,3,2,0,1:T(8,128)S(1)}, bf16[8,2048,1,2,64]{1,4,3,0,2:T(8,128)(2,1)}, bf16[8,2048,1,2]{1,3,0,2:T(2,128)(2,1)S(1)...) while((s32[]{:T(128)}, ...), condition=%wide.region_4.5_spmd.clone, body=%wide.region_1.4_spmd.clone.sunk | while | flops 409817152 | bytes 12787244 | solution.py:47
  355.2 7.1 copy.183
  362.3 11.4 %all-to-all-start.3 = ((bf16[8,2048,128]{2,0,1:T(8,128)(2,1)}), bf16[8,2048,128]{2,0,1:T(8,128)(2,1)}, u32[]{:S(2)}, u32[]{:S(2)}) async-start(bf16[8,2048,128]{2,0,1:T(8,128)(2,1)} %copy.183), calls=%async_computation.3 | async-start | bytes 8388608 | tf_op jit(solution)/shard_map/all_to_all | solution.py:89
  374.5 49.8 %all-to-all-done.3 = bf16[8,2048,128]{2,0,1:T(8,128)(2,1)} async-done(((bf16[8,2048,128]{2,0,1:T(8,128)(2,1)}), bf16[8,2048,128]{2,0,1:T(8,128)(2,1)}, u32[]{:S(2)}, u32[]{:S(2)}) %all-to-all-start.3) | async-done | bytes 4194336 | tf_op jit(solution)/shard_map/all_to_all | solution.py:89
  424.2 2.7 copy.184
  429.0 4.6 multiply_reduce_fusion.1
  433.5 21.3 %multiply_reduce_fusion.2 = (f32[8,64]{1,0:T(8,128)S(1)}, f32[8,64,2048]{2,1,0:T(8,128)}) fusion(f32[8,64,2048]{2,1,0:T(8,128)} %param.14, bf16[2,4096,2048]{2,1,0:T(8,128)(2,1)} %param.23, f32[4096]{0:T(1024)S(1)} %bitcast.433, f32[8,64]{1,0:T(8,128)S(1)} %add_rsqrt_fusion.2, bf16[8,64,8512]{2,1,0:T(8,128)(2,1)} %fusion.114, ...), kind=kOutput, calls=%fused_computation.173 | convolution fusion | flops 8614051840 | bytes 33574912 | tf_op jit(solution)/shard_map/blgc,gcd->bld/dot_general | solution.py:93
  454.9 26.7 %fusion.117 = bf16[8,64,8512]{2,1,0:T(8,128)(2,1)} fusion(bf16[2,2048,8512]{1,2,0:T(8,128)(2,1)} %param.16, f32[8,64,2048]{2,1,0:T(8,128)} %get-tuple-element.503, f32[2048]{0:T(1024)S(1)} %bitcast.436, f32[8,64]{1,0:T(8,128)S(1)} %add_rsqrt_fusion.1), kind=kOutput, calls=%fused_computation.133 | convolution fusion | flops 17858461696 | bytes 47785984 | tf_op jit(solution)/shard_map/bld,de->ble/dot_general | solution.py:69
  483.7 4.7 slice.276
  488.3 4.8 collective-permute-start.1
  495.1 4.6 all-to-all-start.4
  499.8 11.4 %multiply_convert_fusion = bf16[8,64,4352]{2,1,0:T(8,128)(2,1)S(1)} fusion(bf16[8,64,4352]{2,1,0:T(8,128)(2,1)} %slice.276, bf16[8,3,4352]{2,1,0:T(4,128)(2,1)S(1)} %collective-permute-done.1, f32[4352]{0:T(1024)S(1)} %get-tuple-element.439, f32[4352]{0:T(1024)S(1)} %get-tuple-element.440, f32[4352]{0:T(1024)S(1)} %get-tuple-element.441, ...), kind=kLoop, calls=%fused_computation.138 | loop fusion | flops 57933824 | bytes 9208832 | tf_op jit(solution)/shard_map/convert_element_type | solution.py:76
  513.2 2.6 slice.285
  515.9 10.0 %copy.188 = bf16[8,64,4096]{1,0,2:T(8,128)(2,1)} copy(bf16[8,64,4096]{2,1,0:T(8,128)(2,1)} %slice.285) | data formatting | bytes 8388608 | tf_op jit(solution)/shard_map/slice | solution.py:80
  525.8 13.9 %reshape.598 = bf16[32,2,32768]{2,1,0:T(2,128)(2,1)} reshape(bf16[4096,8,64]{2,1,0:T(8,128)(2,1)} %bitcast.405) | data formatting | bytes 8388608
  539.7 6.3 all-to-all-start.5
  547.0 49.5 %all-to-all-done.5 = bf16[32,2,32768]{2,1,0:T(2,128)(2,1)} async-done(((bf16[32,2,32768]{2,1,0:T(2,128)(2,1)}), bf16[32,2,32768]{2,1,0:T(2,128)(2,1)}, u32[]{:S(2)}, u32[]{:S(2)}) %all-to-all-start.5) | async-done | bytes 4194336 | tf_op jit(solution)/shard_map/all_to_all | solution.py:80
  596.5 5.4 reshape.541
  601.9 7.9 all-to-all-start.6
  610.4 13.7 %reshape.599 = bf16[4096,8,64]{2,1,0:T(8,128)(2,1)} reshape(bf16[32,2,32768]{2,1,0:T(2,128)(2,1)} %all-to-all-done.5) | data formatting | bytes 8388608
  624.1 12.0 %copy.250 = bf16[8,64,32,128]{1,2,3,0:T(8,128)(2,1)} copy(bf16[8,64,32,128]{1,0,3,2:T(8,128)(2,1)} %bitcast.408) | data formatting | bytes 8388608 | tf_op jit(solution)/shard_map/all_to_all | solution.py:80
  636.1 12.3 %reshape.539 = bf16[8,2048,1,2,64]{1,4,3,0,2:T(8,128)(2,1)} reshape(bf16[8,32,64,128]{2,1,3,0:T(8,128)(2,1)} %bitcast.409) | data formatting | bytes 8388608 | tf_op jit(solution)/shard_map/reshape | solution.py:87
  648.4 59.6 %all-to-all-done.6 = bf16[8,64,2,32,128]{4,1,0,2,3:T(8,128)(2,1)} async-done(((bf16[8,64,2,32,128]{4,1,0,2,3:T(8,128)(2,1)}), bf16[8,64,2,32,128]{4,1,0,2,3:T(8,128)(2,1)}, u32[]{:S(2)}, u32[]{:S(2)}) %all-to-all-start.6) | async-done | bytes 8388640 | tf_op jit(solution)/shard_map/all_to_all | solution.py:82
  708.0 9.6 copy.191
  720.1 82.5 %while.33 = (s32[]{:T(128)}, f32[8,1,2,64,128]{4,3,2,0,1:T(8,128)S(1)}, bf16[8,2048,1,2,64]{1,4,3,0,2:T(8,128)(2,1)}, bf16[8,2048,1,2]{1,3,0,2:T(2,128)(2,1)S(1)...) while((s32[]{:T(128)}, ...), condition=%wide.region_10.11_spmd.clone, body=%wide.region_7.10_spmd.clone.sunk | while | flops 409817152 | bytes 12787244 | solution.py:47
  802.6 6.9 copy.194
  809.6 11.3 %all-to-all-start.7 = ((bf16[8,2048,128]{2,0,1:T(8,128)(2,1)}), bf16[8,2048,128]{2,0,1:T(8,128)(2,1)}, u32[]{:S(2)}, u32[]{:S(2)}) async-start(bf16[8,2048,128]{2,0,1:T(8,128)(2,1)} %copy.194), calls=%async_computation.7 | async-start | bytes 8388608 | tf_op jit(solution)/shard_map/all_to_all | solution.py:89
  821.7 125.0 %all-reduce.3.cloned.1.call-done = (bf16[8,1,4352,3]{2,3,0,1:T(4,128)(2,1)}, bf16[8,1,4352,3]{2,3,0,1:T(4,128)(2,1)}) async-done(((bf16[8,1,4352,3]{2,3,0,1:T(4,128)(2,1)}, bf16[8,1,4352,3]{2,3,0,1:T(4,128)(2,1)}), (bf16[8,1,4352,3]{2,3,0,1:T(4,128)(2,1)}, bf16[8,1,4352,3]{2,3,0,1:T(4,128)(2,1)})) %all-reduce.3.cloned.1.call-update) | async-done | bytes 417808 | tf_op jit(solution)/shard_map/psum | solution.py:95
  950.5 2.7 copy.195
  955.2 4.6 multiply_reduce_fusion
  959.8 21.4 %fusion.139 = f32[8,64,2048]{2,1,0:T(8,128)} fusion(f32[8,64,2048]{2,1,0:T(8,128)} %get-tuple-element.503, bf16[2,4096,2048]{2,1,0:T(8,128)(2,1)} %param.23, f32[4096]{0:T(1024)S(1)} %bitcast.432, f32[8,64]{1,0:T(8,128)S(1)} %add_rsqrt_fusion, bf16[8,64,8512]{2,1,0:T(8,128)(2,1)} %fusion.117, bf16[8,32,64,128]{3,2,1,0:T(8,128)(2,1)} %bitcast.415), kind=kOutput, calls=%fused_computation.179 | convolution fusion | flops 8611954688 | bytes 33572864 | tf_op jit(solution)/shard_map/blgc,gcd->bld/dot_general | solution.py:93
  (565 shorter events, 197.7 us)
Async XLA Ops:
  11.1 33.2 %copy-start.13 = (f32[2,64]{1,0:T(2,128)S(1)}, f32[2,64]{1,0:T(2,128)}, u32[]{:S(2)}) copy-start(f32[2,64]{1,0:T(2,128)} %param.19) | copy-start | bytes 1540
  37.7 16.7 %copy-start.6 = (f32[2,4352,4]{1,2,0:T(4,128)S(1)}, f32[2,4352,4]{1,2,0:T(4,128)}, u32[]{:S(2)}) copy-start(f32[2,4352,4]{1,2,0:T(4,128)} %param.17) | copy-start | bytes 417796
  37.7 16.8 %copy-start.8 = (f32[2,4352]{1,0:T(2,128)S(1)}, f32[2,4352]{1,0:T(2,128)}, u32[]{:S(2)}) copy-start(f32[2,4352]{1,0:T(2,128)} %param.18) | copy-start | bytes 104452
  39.8 15.6 %collective-permute-start = (bf16[8,3,4352]{2,1,0:T(4,128)(2,1)S(1)}, bf16[8,3,4352]{2,1,0:T(4,128)(2,1)S(1)}, u32[]{:S(2)}, u32[]{:S(2)}) collective-permute-start(bf16[8,3,4352]{2,1,0:T(4,128)(2,1)S(1)} %get-tuple-element.487), channel_id=1, source_target_pairs={{0,1},{1,2},{2,3},{3,4},{4,5},{5,6},{6,7},{7,8},{8,9},{9,10},{10,1... | collective-permute-start | bytes 626696 | tf_op jit(solution)/shard_map/ppermute | solution.py:73
  46.9 45.4 %all-to-all-start = ((bf16[32,2,512]{2,1,0:T(2,128)(2,1)}), bf16[32,2,512]{2,1,0:T(2,128)(2,1)S(1)}, u32[]{:S(2)}, u32[]{:S(2)}) async-start(bf16[32,2,512]{2,1,0:T(2,128)(2,1)} %reshape.592), calls=%async_computation | async-start | bytes 131072 | tf_op jit(solution)/shard_map/all_to_all | solution.py:81
  54.4 2.3 slice-start
  63.8 2.1 copy-start.2
  92.3 56.8 %all-to-all-start.1 = ((bf16[32,2,32768]{2,1,0:T(2,128)(2,1)}), bf16[32,2,32768]{2,1,0:T(2,128)(2,1)}, u32[]{:S(2)}, u32[]{:S(2)}) async-start(bf16[32,2,32768]{2,1,0:T(2,128)(2,1)} %reshape.594), calls=%async_computation.1 | async-start | bytes 8388608 | tf_op jit(solution)/shard_map/all_to_all | solution.py:80
  154.5 7.9 copy-start.14
  154.5 8.5 copy-start.15
  154.5 106.0 %all-to-all-start.2 = ((bf16[8,64,2,32,128]{4,1,0,2,3:T(8,128)(2,1)}), bf16[8,64,2,32,128]{4,1,0,2,3:T(8,128)(2,1)}, u32[]{:S(2)}, u32[]{:S(2)}) async-start(bf16[8,64,2,32,128]{4,1,0,2,3:T(8,128)(2,1)} %reshape.535), calls=%async_computation.2 | async-start | bytes 16777216 | tf_op jit(solution)/shard_map/all_to_all | solution.py:82
  355.2 7.1 copy-start
  355.2 18.7 %copy-start.9 = (f32[2,1,4096]{2,1,0:T(1,128)S(1)}, f32[2,1,4096]{2,1,0:T(1,128)}, u32[]{:S(2)}) copy-start(f32[2,1,4096]{2,1,0:T(1,128)} %param.22) | copy-start | bytes 98308
  362.3 62.0 %all-to-all-start.3 = ((bf16[8,2048,128]{2,0,1:T(8,128)(2,1)}), bf16[8,2048,128]{2,0,1:T(8,128)(2,1)}, u32[]{:S(2)}, u32[]{:S(2)}) async-start(bf16[8,2048,128]{2,0,1:T(8,128)(2,1)} %copy.183), calls=%async_computation.3 | async-start | bytes 8388608 | tf_op jit(solution)/shard_map/all_to_all | solution.py:89
  427.0 2.0 copy-start.4
  433.5 21.3 %copy-start.11 = (f32[1,2048]{1,0:T(1,128)S(1)}, f32[1,2048]{1,0:T(1,128)}, u32[]{:S(2)}) copy-start(f32[1,2048]{1,0:T(1,128)} %get-tuple-element.494) | copy-start | bytes 24580
  481.6 11.5 %copy-start.12 = (f32[64]{0:T(128)S(1)}, f32[64]{0:T(128)}, u32[]{:S(2)}) copy-start(f32[64]{0:T(128)} %get-tuple-element.500) | copy-start | bytes 772
  481.6 18.1 %copy-start.7 = (f32[4352]{0:T(1024)S(1)}, f32[4352]{0:T(1024)}, u32[]{:S(2)}) copy-start(f32[4352]{0:T(1024)} %get-tuple-element.446) | copy-start | bytes 52228
  488.3 11.4 %collective-permute-start.1 = (bf16[8,3,4352]{2,1,0:T(4,128)(2,1)S(1)}, bf16[8,3,4352]{2,1,0:T(4,128)(2,1)S(1)}, u32[]{:S(2)}, u32[]{:S(2)}) collective-permute-start(bf16[8,3,4352]{2,1,0:T(4,128)(2,1)S(1)} %get-tuple-element.489), channel_id=1, source_target_pairs={{0,1},{1,2},{2,3},{3,4},{4,5},{5,6},{6,7},{7,8},{8,9},{9,10},{10,1... | collective-permute-start | bytes 626696 | tf_op jit(solution)/shard_map/ppermute | solution.py:73
  495.1 44.6 %all-to-all-start.4 = ((bf16[32,2,512]{2,1,0:T(2,128)(2,1)}), bf16[32,2,512]{2,1,0:T(2,128)(2,1)S(1)}, u32[]{:S(2)}, u32[]{:S(2)}) async-start(bf16[32,2,512]{2,1,0:T(2,128)(2,1)} %reshape.596), calls=%async_computation.4 | async-start | bytes 131072 | tf_op jit(solution)/shard_map/all_to_all | solution.py:81
  511.2 2.1 copy-start.3
  539.7 56.8 %all-to-all-start.5 = ((bf16[32,2,32768]{2,1,0:T(2,128)(2,1)}), bf16[32,2,32768]{2,1,0:T(2,128)(2,1)}, u32[]{:S(2)}, u32[]{:S(2)}) async-start(bf16[32,2,32768]{2,1,0:T(2,128)(2,1)} %reshape.598), calls=%async_computation.5 | async-start | bytes 8388608 | tf_op jit(solution)/shard_map/all_to_all | solution.py:80
  601.9 7.9 copy-start.16
  601.9 8.0 copy-start.17
  601.9 106.0 %all-to-all-start.6 = ((bf16[8,64,2,32,128]{4,1,0,2,3:T(8,128)(2,1)}), bf16[8,64,2,32,128]{4,1,0,2,3:T(8,128)(2,1)}, u32[]{:S(2)}, u32[]{:S(2)}) async-start(bf16[8,64,2,32,128]{4,1,0,2,3:T(8,128)(2,1)} %reshape.541), calls=%async_computation.6 | async-start | bytes 16777216 | tf_op jit(solution)/shard_map/all_to_all | solution.py:82
  802.6 146.8 %copy-start.1 = (f32[8,1,2,64,128]{4,3,2,0,1:T(8,128)S(1)}, f32[8,1,2,64,128]{4,3,2,0,1:T(8,128)}, u32[]{:S(2)}) copy-start(f32[8,1,2,64,128]{4,3,2,0,1:T(8,128)} %copy-done) | copy-start | bytes 1572868
  809.6 140.9 %all-to-all-start.7 = ((bf16[8,2048,128]{2,0,1:T(8,128)(2,1)}), bf16[8,2048,128]{2,0,1:T(8,128)(2,1)}, u32[]{:S(2)}, u32[]{:S(2)}) async-start(bf16[8,2048,128]{2,0,1:T(8,128)(2,1)} %copy.194), calls=%async_computation.7 | async-start | bytes 8388608 | tf_op jit(solution)/shard_map/all_to_all | solution.py:89
  820.9 125.8 %all-reduce.3.cloned.1.call-start = ((), (), s32[]{:S(2)}) async-start(), calls=%async_computation.8 | async-start | bytes 1114112 | tf_op jit(solution)/shard_map/psum | solution.py:95
  950.5 9.3 copy-start.10
  953.2 2.0 copy-start.5
Sparse Core Ops, SparseCore 0:
  825.8 120.8 all-reduce.2
where the time goes:
time: 1000 us; the launch traced here: 988 us
  waiting for transfers between devices  392 us (39%)
  matrix products  222 us (22%)
  local copies, waits for them, and re-layouts  221 us (22%)
  starting transfers between devices  72.7 us (7%)
  other arithmetic  63.3 us (6%)
  between operations  14.9 us (1%)
    psum x1, waiting for transfers between devices, layer(): conv_state = lax.psum(tail_rows, 'sp')  125 us
    all_to_all x2, waiting for transfers between devices, layer(): bc_local = lax.all_to_all(bc_tokens, 'sp', 3, 1, tiled=True)  118 us
    all_to_all x2, waiting for transfers between devices, layer(): x_local = lax.all_to_all(activated[..., :d_inner], 'sp', 2, 1, tiled=True)  99 us
    unnamed x49, local copies, waits for them, and re-layouts  66.7 us
    dot_general x2, matrix products, layer(): jnp.einsum('bld,de->ble', normed, w_in_l, preferred_element_type=jnp.floa...  53.3 us
    all_to_all x2, waiting for transfers between devices, layer(): lax.all_to_all(y_local.reshape(batch, seq_len, local_heads * head_dim), '...  49.8 us
    dot_general x2, matrix products, layer(): jnp.einsum('blgc,gcd->bld', normed_y, w_out_l.reshape(n_groups, group_wid...  42.7 us
    dot_general x16, matrix products, body(): jnp.einsum('bghts,bsghp->btghp', mix_mat, x_scaled, preferred_element_typ...  37.8 us
  transfers between devices with their start and end apart: 11, of which 6 were waited for; matrix products, arithmetic and copies ran while one was open for 16% of the time, Pallas kernels for 0%

commit v1 on v0

v1 whole, which is shorter than its diff:
```python
import functools

import jax
import jax.numpy as jnp
from jax import lax
from jax.experimental import pallas as pl
from jax.experimental.pallas import tpu as pltpu
from jax.sharding import PartitionSpec as P


CONV_WIDTH = 4
EPSILON = 1e-5
PROMPT_GROUPS = 2
HALO = 8
LANES = 128
NT = (((1,), (1,)), ((), ()))
X_TILE = 512
Z_TILE = 512
OUT_TILE = 512


def silu(values):
    return values * (1.0 / (1.0 + jnp.exp(-values)))


def pick_tile(preferred, total):
    tile = preferred
    while total % tile:
        tile //= 2
    return tile


def xbc_kernel(n_prompts, seg_len, d_inner, d_bc, n_heads, h_ref, halo_ref, w_ref, cw_ref, cb_ref, dtb_ref,
               xs_ref, bc_ref, tail_ref, h_ext, window, turned, dt_rows):
    step = pl.program_id(0)
    rows = n_prompts * seg_len
    tile = w_ref.shape[1]
    pair = LANES // seg_len
    dests = n_heads // pair

    @pl.when(step == 0)
    def _():
        h_ext[:rows] = h_ref[...]
        h_ext[rows:] = halo_ref[...]
        dt_rows[...] = jnp.zeros_like(dt_rows)

    projected = lax.dot_general(h_ext[...], w_ref[0], NT, preferred_element_type=jnp.float32).astype(jnp.bfloat16).astype(jnp.float32)
    window[:, HALO:, :] = projected[:rows].reshape(n_prompts, seg_len, tile)
    window[:, :HALO, :] = projected[rows:].reshape(n_prompts, HALO, tile)
    tail_ref[...] = window[:, seg_len:, :].astype(jnp.bfloat16)

    def convolve(prompt, lane_start, col_start):
        lanes = pl.ds(lane_start, LANES)
        acc = cb_ref[:, pl.ds(col_start, LANES)]
        for tap in range(CONV_WIDTH):
            first = HALO - (CONV_WIDTH - 1) + tap
            acc = acc + window[prompt, first:first + seg_len, lanes] * cw_ref[tap:tap + 1, pl.ds(col_start, LANES)]
        return silu(acc).astype(jnp.bfloat16)

    @pl.when(step == 0)
    def _():
        @pl.loop(0, n_prompts)
        def _(prompt):
            at = pl.ds(pl.multiple_of(prompt * seg_len, seg_len), seg_len)
            for start in range(0, d_bc, LANES):
                bc_ref[at, start:start + LANES] = convolve(prompt, start, d_inner + start)
            raw = window[prompt, HALO:, d_bc:d_bc + LANES] + dtb_ref[...]
            delta = jnp.maximum(raw, 0.0) + jnp.log1p(jnp.exp(-jnp.abs(raw)))
            delta = delta.astype(jnp.bfloat16).astype(jnp.float32)
            turned[...] = jnp.transpose(delta, (1, 0))
            parts = [turned[pl.ds(which, dests, stride=pair), :] for which in range(pair)]
            dt_rows[pl.ds(prompt, dests, stride=HALO), :] = jnp.concatenate(parts, axis=1)

    @pl.when(step > 0)
    def _():
        base = (step - 1) * tile

        @pl.loop(0, n_prompts)
        def _(prompt):
            at = pl.ds(pl.multiple_of(prompt * seg_len, seg_len), seg_len)
            for block in range(tile // LANES):
                start = block * LANES
                xs_ref[block, at, :] = convolve(prompt, start, pl.multiple_of(base + start, LANES))

        for block in range(tile // LANES):
            dest = (step - 1) * (tile // LANES) + block
            xs_ref[block, rows:, :] = dt_rows[pl.ds(pl.multiple_of(dest * HALO, HALO), HALO), :].astype(jnp.bfloat16)


def project_xbc(layer, h, halo, w_in, conv_w, conv_b, dt_bias, n_prompts, seg_len, d_inner, d_bc):
    rows, d_model = h.shape
    n_heads = dt_bias.shape[-1]
    conv_dim = d_inner + d_bc
    tile = pick_tile(X_TILE, d_inner)
    blocks = d_inner // LANES
    x_steps = d_inner // tile
    per = tile // LANES
    m_rows = rows + halo.shape[0]
    bias = jnp.pad(dt_bias[layer][None, :], ((0, 0), (0, LANES - n_heads)))
    x_block = lambda s: jnp.maximum(s - 1, 0)
    col = lambda s: jnp.where(s == 0, x_steps, s - 1)
    whole = lambda *shape: pl.BlockSpec(shape, lambda s: (0,) * len(shape))
    return pl.pallas_call(
        functools.partial(xbc_kernel, n_prompts, seg_len, d_inner, d_bc, n_heads),
        grid=(x_steps + 1,),
        in_specs=[whole(rows, d_model), whole(*halo.shape),
                  pl.BlockSpec((1, tile, d_model), lambda s: (layer, d_inner // tile + col(s), 0)),
                  whole(CONV_WIDTH, conv_dim), whole(1, conv_dim), whole(1, LANES)],
        out_specs=[pl.BlockSpec((per, rows + HALO, LANES), lambda s: (x_block(s), 0, 0)),
                   whole(rows, d_bc),
                   pl.BlockSpec((n_prompts, HALO, tile), lambda s: (0, 0, col(s)))],
        out_shape=[jax.ShapeDtypeStruct((blocks, rows + HALO, LANES), jnp.bfloat16),
                   jax.ShapeDtypeStruct((rows, d_bc), jnp.bfloat16),
                   jax.ShapeDtypeStruct((n_prompts, HALO, conv_dim), jnp.bfloat16)],
        scratch_shapes=[pltpu.VMEM((m_rows, d_model), jnp.bfloat16),
                        pltpu.VMEM((n_prompts, seg_len + HALO, tile), jnp.float32),
                        pltpu.VMEM((LANES, seg_len), jnp.float32),
                        pltpu.VMEM((blocks * HALO, LANES), jnp.float32)],
        cost_estimate=pl.CostEstimate(flops=2 * m_rows * d_model * (conv_dim + n_heads), bytes_accessed=2 * d_model * (conv_dim + n_heads), transcendentals=0),
    )(h, halo, w_in, conv_w, conv_b, bias)


def z_kernel(h_ref, w_ref, z_ref):
    z_ref[...] = lax.dot_general(h_ref[...], w_ref[0], NT, preferred_element_type=jnp.float32).astype(jnp.bfloat16)


def project_z(layer, h, w_in, d_inner):
    rows, d_model = h.shape
    tile = pick_tile(Z_TILE, d_inner)
    return pl.pallas_call(
        z_kernel,
        grid=(d_inner // tile,),
        in_specs=[pl.BlockSpec((rows, d_model), lambda s: (0, 0)),
                  pl.BlockSpec((1, tile, d_model), lambda s: (layer, s, 0))],
        out_specs=pl.BlockSpec((rows, tile), lambda s: (0, s)),
        out_shape=jax.ShapeDtypeStruct((rows, d_inner), jnp.bfloat16),
        cost_estimate=pl.CostEstimate(flops=2 * rows * d_model * d_inner, bytes_accessed=2 * d_model * d_inner, transcendentals=0),
    )(h, w_in)


def scan_kernel(n_prompts, seg_len, segs, head_dim, d_state, x_ref, bc_ref, a_ref, d_ref, y_ref, state_ref,
                row_refs, col_ref, dtc_ref):
    chunk = segs * seg_len
    rows = n_prompts * seg_len
    heads = LANES // head_dim

    @pl.when(pl.program_id(0) == 0)
    def _():
        state_ref[...] = jnp.zeros_like(state_ref)

    token_r = lax.broadcasted_iota(jnp.int32, (chunk, chunk), 0)
    token_c = lax.broadcasted_iota(jnp.int32, (chunk, chunk), 1)
    causal = token_r >= token_c
    lower = causal.astype(jnp.float32)
    upper = (token_r <= token_c).astype(jnp.float32)
    eye = (token_r == token_c).astype(jnp.float32)
    nt = (((1,), (1,)), ((), ()))
    tn = (((0,), (0,)), ((), ()))

    per_seg = [x_ref[seg, rows:, :].astype(jnp.float32) for seg in range(segs)]
    steps = jnp.concatenate([jnp.concatenate([part[:, head * seg_len:(head + 1) * seg_len] for part in per_seg], axis=1)
                             for head in range(heads)], axis=0)
    row_refs[...] = jnp.dot(steps, upper, preferred_element_type=jnp.float32)
    col_ref[...] = lax.dot_general(lower, steps, nt, preferred_element_type=jnp.float32)
    dtc_ref[...] = lax.dot_general(eye, steps, nt, preferred_element_type=jnp.float32)

    lane = lax.broadcasted_iota(jnp.int32, (chunk, LANES), 1)
    state_row = lax.broadcasted_iota(jnp.int32, (LANES, d_state), 0)
    pick = lax.broadcasted_iota(jnp.int32, (chunk, heads * HALO), 1)

    @pl.loop(0, n_prompts)
    def _(prompt):
        at = pl.ds(pl.multiple_of(prompt * seg_len, seg_len), seg_len)
        x_float = x_ref[:, at, :].reshape(chunk, LANES).astype(jnp.float32)
        b_part = bc_ref[:, at, :d_state].reshape(chunk, d_state)
        c_part = bc_ref[:, at, d_state:].reshape(chunk, d_state)
        scores = lax.dot_general(c_part, b_part, nt, preferred_element_type=jnp.float32)
        state = state_ref[prompt]
        y_inter = lax.dot_general(c_part.astype(jnp.float32), state, nt, preferred_element_type=jnp.float32)

        cums = [jnp.sum(jnp.where(pick == head * HALO + prompt, col_ref[...], 0.0), axis=1, keepdims=True) for head in range(heads)]
        dts = [jnp.sum(jnp.where(pick == head * HALO + prompt, dtc_ref[...], 0.0), axis=1, keepdims=True) for head in range(heads)]
        cum_log = jnp.broadcast_to(cums[0] * a_ref[0], (chunk, LANES))
        delta = jnp.broadcast_to(dts[0], (chunk, LANES))
        for head in range(1, heads):
            cum_log = jnp.where(lane >= head * head_dim, cums[head] * a_ref[head], cum_log)
            delta = jnp.where(lane >= head * head_dim, dts[head], delta)
        x_scaled = x_float * delta
        skip = jnp.broadcast_to(d_ref[0], (chunk, LANES))
        for head in range(1, heads):
            skip = jnp.where(lane >= head * head_dim, d_ref[head], skip)

        y_value = y_inter * jnp.exp(cum_log) + skip * x_float
        kept = jnp.zeros((LANES, d_state), jnp.float32)
        for head in range(heads):
            row = row_refs[pl.ds(head * HALO + prompt, 1), :]
            decay = jnp.exp(jnp.where(causal, (cums[head] - row) * a_ref[head], -jnp.inf))
            mine = (lane >= head * head_dim) & (lane < (head + 1) * head_dim)
            y_value = y_value + jnp.dot(decay * scores, jnp.where(mine, x_scaled, 0.0), preferred_element_type=jnp.float32)
            last = jnp.exp(cums[head][chunk - 1:chunk] * a_ref[head])
            kept = jnp.where(state_row >= head * head_dim, last, kept)
        x_left = x_scaled * jnp.exp(cum_log[chunk - 1:chunk] - cum_log)
        state_ref[prompt] = state * kept + lax.dot_general(x_left, b_part.astype(jnp.float32), tn, preferred_element_type=jnp.float32)
        y_ref[:, at, :] = y_value.astype(jnp.bfloat16).reshape(segs, seg_len, LANES)


def scan_heads(x_recv, bc_all, a_neg, d_vec, n_prompts, seg_len, head_dim, d_state):
    seg_count, rows_x, _ = x_recv.shape
    rows = n_prompts * seg_len
    heads = LANES // head_dim
    segs = 4
    while seg_count % segs:
        segs //= 2
    chunk = segs * seg_len
    steps = seg_count // segs
    flops = steps * n_prompts * 2 * chunk * LANES * (chunk * (1 + heads) + 2 * d_state)
    return pl.pallas_call(
        functools.partial(scan_kernel, n_prompts, seg_len, segs, head_dim, d_state),
        grid=(steps,),
        in_specs=[pl.BlockSpec((segs, rows_x, LANES), lambda s: (s, 0, 0)),
                  pl.BlockSpec((segs, rows, 2 * d_state), lambda s: (s, 0, 0)),
                  pl.BlockSpec(memory_space=pltpu.SMEM),
                  pl.BlockSpec(memory_space=pltpu.SMEM)],
        out_specs=[pl.BlockSpec((segs, rows, LANES), lambda s: (s, 0, 0)),
                   pl.BlockSpec((n_prompts, LANES, d_state), lambda s: (0, 0, 0))],
        out_shape=[jax.ShapeDtypeStruct((seg_count, rows, LANES), jnp.bfloat16),
                   jax.ShapeDtypeStruct((n_prompts, LANES, d_state), jnp.float32)],
        scratch_shapes=[pltpu.VMEM((heads * HALO, chunk), jnp.float32),
                        pltpu.VMEM((chunk, heads * HALO), jnp.float32),
                        pltpu.VMEM((chunk, heads * HALO), jnp.float32)],
        cost_estimate=pl.CostEstimate(flops=flops * 4, bytes_accessed=seg_count * rows * 2 * (2 * LANES + 2 * d_state), transcendentals=0),
    )(x_recv, bc_all, a_neg, d_vec)


def out_kernel(with_next, n_tiles, y_ref, z_ref, gate_ref, w_ref, resid_ref, pre_ref, *rest):
    if with_next:
        out_ref, h_ref, normed, gated, kept = rest
    else:
        out_ref, normed, gated = rest[-3:]
    step = pl.program_id(0)
    blocks, rows, _ = y_ref.shape
    part = gated.shape[0]
    tile = out_ref.shape[-1]

    @pl.when(step == 0)
    def _():
        @pl.loop(0, rows // part)
        def _(index):
            at = pl.ds(pl.multiple_of(index * part, part), part)
            total = jnp.zeros((part, LANES), jnp.float32)
            for block in range(blocks):
                lanes = slice(block * LANES, (block + 1) * LANES)
                value = y_ref[block, at, :].astype(jnp.float32) * silu(z_ref[at, lanes].astype(jnp.float32))
                total = total + value * value
                gated[:, lanes] = value
            mean_sq = jnp.sum(total, axis=1, keepdims=True) * (1.0 / (blocks * LANES))
            scale = lax.rsqrt(mean_sq + EPSILON)
            for block in range(blocks):
                lanes = slice(block * LANES, (block + 1) * LANES)
                normed[at, lanes] = (gated[:, lanes] * scale * gate_ref[:, lanes]).astype(jnp.bfloat16)

    value = resid_ref[...] + jnp.dot(normed[...], w_ref[0], preferred_element_type=jnp.float32)
    out_ref[...] = value
    if with_next:
        kept[:, pl.ds(pl.multiple_of(step * tile, tile), tile)] = value

        @pl.when(step == n_tiles - 1)
        def _():
            @pl.loop(0, rows // part)
            def _(index):
                at = pl.ds(pl.multiple_of(index * part, part), part)
                row = kept[at, :]
                mean_sq = jnp.mean(row * row, axis=1, keepdims=True)
                h_ref[at, :] = (row * lax.rsqrt(mean_sq + EPSILON) * pre_ref[...]).astype(jnp.bfloat16)


def project_out(layer, y_recv, z, gate_w, w_out, resid, resid_block, next_pre, shared=None, out_block=0, out_rows=None):
    blocks, rows, _ = y_recv.shape
    d_inner = blocks * LANES
    d_model = resid.shape[-1]
    tile = pick_tile(OUT_TILE, d_model)
    n_tiles = d_model // tile
    with_next = next_pre is not None
    part = min(32, rows)
    whole = lambda *shape: pl.BlockSpec(shape, lambda s: (0,) * len(shape), pipeline_mode=pl.Buffered(1))
    out_specs = [pl.BlockSpec((rows, tile), lambda s: (out_block, s))]
    out_shape = [jax.ShapeDtypeStruct((out_rows or rows, d_model), jnp.float32)]
    scratch = [pltpu.VMEM((rows, d_inner), jnp.bfloat16), pltpu.VMEM((part, d_inner), jnp.float32)]
    if with_next:
        out_specs.append(pl.BlockSpec((rows, d_model), lambda s: (0, 0)))
        out_shape.append(jax.ShapeDtypeStruct((rows, d_model), jnp.bfloat16))
        scratch.append(pltpu.VMEM((rows, d_model), jnp.float32))
    else:
        next_pre = gate_w[:, :d_model]
    extra = [] if shared is None else [shared]
    result = pl.pallas_call(
        functools.partial(out_kernel, with_next, n_tiles),
        grid=(n_tiles,),
        in_specs=[whole(blocks, rows, LANES), whole(rows, d_inner), whole(1, d_inner),
                  pl.BlockSpec((1, d_inner, tile), lambda s: (layer, 0, s)),
                  pl.BlockSpec((rows, tile), lambda s: (resid_block, s)), whole(1, d_model)] + [pl.BlockSpec(memory_space=pl.ANY)] * len(extra),
        input_output_aliases={6: 0} if extra else {},
        out_specs=out_specs,
        out_shape=out_shape,
        scratch_shapes=scratch,
        cost_estimate=pl.CostEstimate(flops=2 * rows * d_inner * d_model, bytes_accessed=2 * d_inner * d_model, transcendentals=0),
    )(y_recv, z, gate_w, w_out, resid, next_pre, *extra)
    return (result[0], result[1]) if with_next else (result[0], None)


def solution(mesh):
    seg_count = mesh.shape['sp']

    def step(resid, pre_norm, w_in, conv_w, conv_b, dt_bias, a_log, d_skip, gate_norm, w_out):
        batch, seg_len, d_model = resid.shape
        n_layers, n_groups, group_width = gate_norm.shape
        d_inner = n_groups * group_width
        n_heads = dt_bias.shape[1]
        conv_dim = conv_b.shape[1]
        d_bc = conv_dim - d_inner
        d_state = d_bc // (2 * n_groups)
        head_dim = d_inner // n_heads
        local_heads = n_heads // seg_count
        assert n_groups == 1 and local_heads * head_dim == LANES
        seg_index = lax.axis_index('sp')
        n_prompts = batch // PROMPT_GROUPS
        rows = n_prompts * seg_len
        taps = jnp.swapaxes(conv_w, 1, 2)
        a_neg = -jnp.exp(lax.dynamic_slice_in_dim(a_log, seg_index * local_heads, local_heads, axis=1))
        d_local = lax.dynamic_slice_in_dim(d_skip, seg_index * local_heads, local_heads, axis=1)
        hops = [(source, source + 1) for source in range(seg_count - 1)]

        w_rows = jnp.swapaxes(w_in, 1, 2)
        whole_resid = resid.reshape(batch * seg_len, d_model)
        streams = []
        for group in range(PROMPT_GROUPS):
            part = whole_resid[group * rows:(group + 1) * rows]
            mean_sq = jnp.mean(part * part, axis=-1, keepdims=True)
            h = (part * lax.rsqrt(mean_sq + EPSILON) * pre_norm[0]).astype(jnp.bfloat16)
            streams.append((whole_resid, group, h))

        finals = []
        tails = []
        summed = None
        for layer in range(n_layers):
            final_layer = layer + 1 == n_layers
            layer_finals = []
            sent = []
            for _, _, h in streams:
                edge = h.reshape(n_prompts, seg_len, d_model)[:, seg_len - HALO:].reshape(n_prompts * HALO, d_model)
                halo = lax.ppermute(edge, 'sp', hops)
                sent.append(project_xbc(layer, h, halo, w_rows, taps[layer], conv_b[layer][None, :], dt_bias, n_prompts, seg_len, d_inner, d_bc))
            tail = jnp.concatenate([item[2][:, HALO - (CONV_WIDTH - 1):] for item in sent], axis=0)
            tail = jnp.where(seg_index == seg_count - 1, tail, jnp.zeros((), jnp.bfloat16)).reshape(batch * (CONV_WIDTH - 1), conv_dim)
            if summed is not None:
                tail, summed = lax.optimization_barrier((tail, summed))
                tails[-1] = summed
            summed = lax.optimization_barrier(lax.psum(tail, 'sp'))
            tails.append(summed)
            gates = []
            arrived = []
            for group, (_, _, h) in enumerate(streams):
                x_send, bc, _ = sent[group]
                x_recv = lax.all_to_all(x_send, 'sp', 0, 0, tiled=True)
                bc_all = lax.all_gather(bc, 'sp', axis=0)
                arrived.append((x_recv, bc_all))
                gates.append(project_z(layer, h, w_rows, d_inner))
            next_streams = []
            shared = None
            for group, (part, block, h) in enumerate(streams):
                x_recv, bc_all = arrived[group]
                if group == 0:
                    bc_all, tail = lax.optimization_barrier((bc_all, tail))
                y_send, final = scan_heads(x_recv, bc_all, a_neg[layer], d_local[layer], n_prompts, seg_len, head_dim, d_state)
                layer_finals.append(final.reshape(n_prompts, local_heads, head_dim, d_state))
                y_recv = lax.all_to_all(y_send, 'sp', 0, 0, tiled=True)
                if final_layer:
                    shared, _ = project_out(layer, y_recv, gates[group], gate_norm[layer], w_out, part, block, None, shared, group, batch * seg_len)
                else:
                    new_part, new_h = project_out(layer, y_recv, gates[group], gate_norm[layer], w_out, part, block, pre_norm[layer + 1][None, :])
                    next_streams.append((new_part, 0, new_h))
            streams = next_streams
            finals.append(jnp.concatenate(layer_finals, axis=0))
        states = [jnp.swapaxes(tail.reshape(batch, CONV_WIDTH - 1, conv_dim), 1, 2) for tail in tails]
        return shared.reshape(batch, seg_len, d_model), jnp.stack(finals, axis=1), jnp.stack(states, axis=1)

    return jax.shard_map(step, mesh=mesh, in_specs=(P('dp', 'sp', None), P(), P(), P(), P(), P(), P(), P(), P(), P()), out_specs=(P('dp', 'sp', None), P('dp', None, 'sp', None, None), P('dp', None, None, None)), check_vma=False)
```

time: 1000 us -> 606 us (0.61)
  Pallas kernels: 0 us -> 251 us
  matrix products: 222 us -> 0 us
  local copies, waits for them, and re-layouts: 221 us -> 21.8 us
  waiting for transfers between devices: 392 us -> 194 us
  blocking collectives: 0 us -> 73 us
  other arithmetic: 63.3 us -> 8.09 us
  starting transfers between devices: 72.7 us -> 41.2 us
    pallas_call x0 -> x16, Pallas kernels: none -> 251 us  [the longest x4 77.6 us: scan_heads(): pl.pallas_call(functools.partial(scan_kernel, n_prompts, seg_len, segs, h...]
    dot_general x68 -> x0, matrix products: 222 us -> none  [the longest x2 53.3 us: layer(): jnp.einsum('bld,de->ble', normed, w_in_l, preferred_element_type=jnp.floa...]
    all_to_all x8 -> x6, waiting for transfers between devices: 267 us -> 66.2 us  [the longest x4 49.5 us: step(): y_recv = lax.all_to_all(y_send, 'sp', 0, 0, tiled=True)]
    all_to_all x0 -> x2, blocking collectives: none -> 73 us  [step(): x_recv = lax.all_to_all(x_send, 'sp', 0, 0, tiled=True)]
    unnamed x49 -> x59, local copies, waits for them, and re-layouts: 66.7 us -> 11 us
    all_to_all x6 -> x0, local copies, waits for them, and re-layouts: 48.8 us -> none  [the longest x2 24 us: layer(): x_local = lax.all_to_all(activated[..., :d_inner], 'sp', 2, 1, tiled=True)]
    reshape x8 -> x4, local copies, waits for them, and re-layouts: 51.5 us -> 2.96 us  [the longest x2 1.83 us: step(): h.reshape(n_prompts, seg_len, d_model)[:, seg_len - HALO:]]
    slice x46 -> x10, local copies, waits for them, and re-layouts: 38.1 us -> 2.34 us  [the longest x1 0.67 us: step(): pre_norm[layer + 1][None, :]]
  transfers between devices with their start and end apart: 11 -> 16, of which waited for: 6 -> 10; matrix products, arithmetic and copies ran while one was open for 16% -> 3% of each run, Pallas kernels for 0% -> 37%
where the time goes in v1:
time: 606 us; the launch traced here: 604 us
  Pallas kernels  251 us (41%)
  waiting for transfers between devices  194 us (32%)
  blocking collectives  73 us (12%)
  starting transfers between devices  41.2 us (7%)
  local copies, waits for them, and re-layouts  21.8 us (4%)
  between operations  14.5 us (2%)
  other arithmetic  8.09 us (1%)
    psum x2, waiting for transfers between devices, step(): summed = lax.optimization_barrier(lax.psum(tail, 'sp'))  91.7 us
    pallas_call x4, Pallas kernels, scan_heads(): pl.pallas_call(functools.partial(scan_kernel, n_prompts, seg_len, segs, h...  77.6 us
    all_to_all x2, blocking collectives, step(): x_recv = lax.all_to_all(x_send, 'sp', 0, 0, tiled=True)  73 us
    pallas_call x4, Pallas kernels, project_xbc(): pl.pallas_call(functools.partial(xbc_kernel, n_prompts, seg_len, d_inner,...  67.8 us
    pallas_call x4, Pallas kernels, project_out(): pl.pallas_call(functools.partial(out_kernel, with_next, n_tiles), grid=(n...  57.9 us
    all_to_all x4, waiting for transfers between devices, step(): y_recv = lax.all_to_all(y_send, 'sp', 0, 0, tiled=True)  49.5 us
    pallas_call x4, Pallas kernels, project_z(): pl.pallas_call(z_kernel, grid=(d_inner // tile,), in_specs=[pl.BlockSpec(...  48.1 us
    all_gather x4, waiting for transfers between devices, step(): bc_all = lax.all_gather(bc, 'sp', axis=0)  30 us
  transfers between devices with their start and end apart: 16, of which 10 were waited for; matrix products, arithmetic and copies ran while one was open for 3% of the time, Pallas kernels for 37%

profile of v1, /device:TPU:97, one launch (start us, length us, event | category | flops | bytes accessed | tf_op | source)
XLA Modules:
  0.0 603.5 jit_solution(17587564501835401029)
XLA Ops:
  7.3 2.7 multiply_reduce_fusion
  11.5 4.6 collective-permute-start.2
  17.5 3.6 fusion.1
  22.3 16.9 %shard_map.128 = (bf16[32,264,128]{2,1,0:T(8,128)(2,1)}, bf16[256,256]{1,0:T(8,128)(2,1)}, bf16[4,8,4352]{2,1,0:T(8,128)(2,1)}) custom-call(bf16[256,2048]{1,0:T(8,128)(2,1)} %get-tuple-element.76.h_ref, bf16[32,2048]{1,0:T(8,128)(2,1)} %copy-done.15, bf16[2,8512,2048]{2,1,0:T(8,128)(2,1)} %bitcast.3.w_ref, f32[4,4352]{1,0:T(4,128)} %get-tuple-element.67.cw_ref, ...), custom_call_target="tpu_custom_call" | custom-call | flops 5209325568 | bytes 18087936 | tf_op jit(solution)/shard_map/pallas_call | solution.py:103
  39.3 2.0 collective-permute-start
  41.3 1.9 collective-permute-done.halo_ref
  43.9 16.9 %shard_map.121 = (bf16[32,264,128]{2,1,0:T(8,128)(2,1)}, bf16[256,256]{1,0:T(8,128)(2,1)}, bf16[4,8,4352]{2,1,0:T(8,128)(2,1)}) custom-call(bf16[256,2048]{1,0:T(8,128)(2,1)} %get-tuple-element.77.h_ref, bf16[32,2048]{1,0:T(8,128)(2,1)} %copy-done.17, bf16[2,8512,2048]{2,1,0:T(8,128)(2,1)} %bitcast.3.w_ref, f32[4,4352]{1,0:T(4,128)} %get-tuple-element.67.cw_ref, ...), custom_call_target="tpu_custom_call" | custom-call | flops 5209325568 | bytes 18087936 | tf_op jit(solution)/shard_map/pallas_call | solution.py:103
  60.9 9.2 %all-to-all-start.4 = ((bf16[32,264,128]{2,1,0:T(8,128)(2,1)}), bf16[32,264,128]{2,1,0:T(8,128)(2,1)S(1)}, u32[]{:S(2)}, u32[]{:S(2)}) async-start(bf16[32,264,128]{2,1,0:T(8,128)(2,1)} %get-tuple-element.39), calls=%async_computation.4 | async-start | bytes 4325376 | tf_op jit(solution)/shard_map/all_to_all | solution.py:364
  72.5 30.0 %all-gather.13.cloned.1.call-done = bf16[8192,256]{1,0:T(8,128)(2,1)} async-done(((bf16[256,256]{1,0:T(8,128)(2,1)}), bf16[8192,256]{1,0:T(8,128)(2,1)}) %all-gather.13.cloned.1.call-update) | async-done | bytes 4194320 | tf_op jit(solution)/shard_map/all_gather | solution.py:365
  102.5 1.1 all-to-all-done.4.x_ref
  103.6 1.3 copy-done.6
  105.0 19.4 %shard_map.129 = (bf16[32,256,128]{2,1,0:T(8,128)(2,1)}, f32[4,128,128]{2,1,0:T(8,128)}) custom-call(bf16[32,264,128]{2,1,0:T(8,128)(2,1)} %copy-done.6, bf16[32,256,256]{2,1,0:T(8,128)(2,1)} %bitcast.81, f32[2]{0:T(128)} %get-tuple-element.81.a_ref, f32[2]{0:T(128)} %get-tuple-element.79.d_ref), custom_call_target="tpu_custom_call" | custom-call | flops 8589934592 | bytes 8388608 | tf_op jit(solution)/shard_map/pallas_call | solution.py:217
  124.4 3.9 all-to-all-start.5
  128.4 12.3 %shard_map.130.z_ref = bf16[256,4096]{1,0:T(8,128)(2,1)} custom-call(bf16[256,2048]{1,0:T(8,128)(2,1)} %get-tuple-element.76.h_ref, bf16[2,8512,2048]{2,1,0:T(8,128)(2,1)} %bitcast.3.w_ref), custom_call_target="tpu_custom_call" | custom-call | flops 4294967296 | bytes 16777216 | tf_op jit(solution)/shard_map/pallas_call | solution.py:130
  141.3 24.2 %all-to-all-done.5.y_ref = bf16[32,256,128]{2,1,0:T(8,128)(2,1)S(1)} async-done(((bf16[32,256,128]{2,1,0:T(8,128)(2,1)}), bf16[32,256,128]{2,1,0:T(8,128)(2,1)S(1)}, u32[]{:S(2)}, u32[]{:S(2)}) %all-to-all-start.5) | async-done | bytes 2097184 | tf_op jit(solution)/shard_map/all_to_all | solution.py:376
  165.4 1.4 copy-done.2
  166.8 15.2 %shard_map.131 = (f32[256,2048]{1,0:T(8,128)}, bf16[256,2048]{1,0:T(8,128)(2,1)}) custom-call(bf16[32,256,128]{2,1,0:T(8,128)(2,1)} %copy-done.2, bf16[256,4096]{1,0:T(8,128)(2,1)} %shard_map.130.z_ref, f32[1,4096]{1,0:T(1,128)} %get-tuple-element.71.gate_ref, bf16[2,4096,2048]{2,1,0:T(8,128)(2,1)} %w_ref.7, f32[512,2048]{1,0:T(8,128)} %bitcast.63, ...), custom_call_target="tpu_custom_call" | custom-call | flops 4294967296 | bytes 16777216 | tf_op jit(solution)/shard_map/pallas_call | solution.py:296
  182.9 2.6 collective-permute-start.3
  186.2 1.2 collective-permute-done.3.halo_ref
  188.1 17.0 %shard_map.132 = (bf16[32,264,128]{2,1,0:T(8,128)(2,1)}, bf16[256,256]{1,0:T(8,128)(2,1)}, bf16[4,8,4352]{2,1,0:T(8,128)(2,1)}) custom-call(bf16[256,2048]{1,0:T(8,128)(2,1)} %get-tuple-element.45.h_ref, bf16[32,2048]{1,0:T(8,128)(2,1)} %copy-done.16, bf16[2,8512,2048]{2,1,0:T(8,128)(2,1)} %bitcast.3.w_ref, f32[4,4352]{1,0:T(4,128)} %get-tuple-element.66.cw_ref, ...), custom_call_target="tpu_custom_call" | custom-call | flops 5209325568 | bytes 18087936 | tf_op jit(solution)/shard_map/pallas_call | solution.py:103
  205.2 34.9 %all_to_all.40.x_ref = bf16[32,264,128]{2,1,0:T(8,128)(2,1)} all-to-all(bf16[32,264,128]{2,1,0:T(8,128)(2,1)S(1)} %copy-done.4), channel_id=1, replica_groups=mesh['dp'=1,'sp'=32] {'sp'}, dimensions={0} | all-to-all | bytes 4325376 | tf_op jit(solution)/shard_map/all_to_all | solution.py:364
  240.1 19.4 %shard_map.122 = (bf16[32,256,128]{2,1,0:T(8,128)(2,1)}, f32[4,128,128]{2,1,0:T(8,128)}) custom-call(bf16[32,264,128]{2,1,0:T(8,128)(2,1)} %all_to_all.40.x_ref, bf16[32,256,256]{2,1,0:T(8,128)(2,1)} %bitcast.79, f32[2]{0:T(128)} %get-tuple-element.81.a_ref, f32[2]{0:T(128)} %get-tuple-element.79.d_ref), custom_call_target="tpu_custom_call" | custom-call | flops 8589934592 | bytes 8388608 | tf_op jit(solution)/shard_map/pallas_call | solution.py:217
  259.5 3.0 all-to-all-start.1
  262.7 11.9 %shard_map.123.z_ref = bf16[256,4096]{1,0:T(8,128)(2,1)} custom-call(bf16[256,2048]{1,0:T(8,128)(2,1)} %get-tuple-element.77.h_ref, bf16[2,8512,2048]{2,1,0:T(8,128)(2,1)} %bitcast.3.w_ref), custom_call_target="tpu_custom_call" | custom-call | flops 4294967296 | bytes 16777216 | tf_op jit(solution)/shard_map/pallas_call | solution.py:130
  274.7 16.5 %all-to-all-done.1.y_ref = bf16[32,256,128]{2,1,0:T(8,128)(2,1)S(1)} async-done(((bf16[32,256,128]{2,1,0:T(8,128)(2,1)}), bf16[32,256,128]{2,1,0:T(8,128)(2,1)S(1)}, u32[]{:S(2)}, u32[]{:S(2)}) %all-to-all-start.1) | async-done | bytes 2097184 | tf_op jit(solution)/shard_map/all_to_all | solution.py:376
  291.2 1.3 copy-done.3
  292.6 15.2 %shard_map.124 = (f32[256,2048]{1,0:T(8,128)}, bf16[256,2048]{1,0:T(8,128)(2,1)}) custom-call(bf16[32,256,128]{2,1,0:T(8,128)(2,1)} %copy-done.3, bf16[256,4096]{1,0:T(8,128)(2,1)} %shard_map.123.z_ref, f32[1,4096]{1,0:T(1,128)} %get-tuple-element.71.gate_ref, bf16[2,4096,2048]{2,1,0:T(8,128)(2,1)} %w_ref.7, f32[512,2048]{1,0:T(8,128)} %bitcast.64, ...), custom_call_target="tpu_custom_call" | custom-call | flops 4294967296 | bytes 16777216 | tf_op jit(solution)/shard_map/pallas_call | solution.py:296
  308.7 3.5 collective-permute-start.1
  312.2 2.2 collective-permute-done.1.halo_ref
  315.0 17.0 %shard_map.125 = (bf16[32,264,128]{2,1,0:T(8,128)(2,1)}, bf16[256,256]{1,0:T(8,128)(2,1)}, bf16[4,8,4352]{2,1,0:T(8,128)(2,1)}) custom-call(bf16[256,2048]{1,0:T(8,128)(2,1)} %get-tuple-element.34.h_ref, bf16[32,2048]{1,0:T(8,128)(2,1)} %copy-done.18, bf16[2,8512,2048]{2,1,0:T(8,128)(2,1)} %bitcast.3.w_ref, f32[4,4352]{1,0:T(4,128)} %get-tuple-element.66.cw_ref, ...), custom_call_target="tpu_custom_call" | custom-call | flops 5209325568 | bytes 18087936 | tf_op jit(solution)/shard_map/pallas_call | solution.py:103
  332.0 38.2 %all_to_all.41.x_ref = bf16[32,264,128]{2,1,0:T(8,128)(2,1)} all-to-all(bf16[32,264,128]{2,1,0:T(8,128)(2,1)S(1)} %copy-done.5), channel_id=1, replica_groups=mesh['dp'=1,'sp'=32] {'sp'}, dimensions={0} | all-to-all | bytes 4325376 | tf_op jit(solution)/shard_map/all_to_all | solution.py:364
  370.2 3.2 all-to-all-start.2
  374.7 19.4 %shard_map.133 = (bf16[32,256,128]{2,1,0:T(8,128)(2,1)}, f32[4,128,128]{2,1,0:T(8,128)}) custom-call(bf16[32,264,128]{2,1,0:T(8,128)(2,1)} %all_to_all.41.x_ref, bf16[32,256,256]{2,1,0:T(8,128)(2,1)} %bitcast.80, f32[2]{0:T(128)} %get-tuple-element.80.a_ref, f32[2]{0:T(128)} %get-tuple-element.78.d_ref), custom_call_target="tpu_custom_call" | custom-call | flops 8589934592 | bytes 8388608 | tf_op jit(solution)/shard_map/pallas_call | solution.py:217
  394.1 15.6 %all-to-all-done.2.x_ref = bf16[32,264,128]{2,1,0:T(8,128)(2,1)S(1)} async-done(((bf16[32,264,128]{2,1,0:T(8,128)(2,1)}), bf16[32,264,128]{2,1,0:T(8,128)(2,1)S(1)}, u32[]{:S(2)}, u32[]{:S(2)}) %all-to-all-start.2) | async-done | bytes 2162720 | tf_op jit(solution)/shard_map/all_to_all | solution.py:364
  409.7 1.3 copy-done.7
  411.1 3.7 all-to-all-start.7
  415.4 19.4 %shard_map.126 = (bf16[32,256,128]{2,1,0:T(8,128)(2,1)}, f32[4,128,128]{2,1,0:T(8,128)}) custom-call(bf16[32,264,128]{2,1,0:T(8,128)(2,1)} %copy-done.7, bf16[32,256,256]{2,1,0:T(8,128)(2,1)} %bitcast.82, f32[2]{0:T(128)} %get-tuple-element.80.a_ref, f32[2]{0:T(128)} %get-tuple-element.78.d_ref), custom_call_target="tpu_custom_call" | custom-call | flops 8589934592 | bytes 8388608 | tf_op jit(solution)/shard_map/pallas_call | solution.py:217
  434.8 8.8 %all-to-all-done.7.y_ref = bf16[32,256,128]{2,1,0:T(8,128)(2,1)S(1)} async-done(((bf16[32,256,128]{2,1,0:T(8,128)(2,1)}), bf16[32,256,128]{2,1,0:T(8,128)(2,1)S(1)}, u32[]{:S(2)}, u32[]{:S(2)}) %all-to-all-start.7) | async-done | bytes 2097184 | tf_op jit(solution)/shard_map/all_to_all | solution.py:376
  443.6 1.4 copy-done.1
  445.0 5.0 all-to-all-start.3
  450.1 11.9 %shard_map.134.z_ref = bf16[256,4096]{1,0:T(8,128)(2,1)} custom-call(bf16[256,2048]{1,0:T(8,128)(2,1)} %get-tuple-element.45.h_ref, bf16[2,8512,2048]{2,1,0:T(8,128)(2,1)} %bitcast.3.w_ref), custom_call_target="tpu_custom_call" | custom-call | flops 4294967296 | bytes 16777216 | tf_op jit(solution)/shard_map/pallas_call | solution.py:130
  462.0 12.0 %shard_map.127.z_ref = bf16[256,4096]{1,0:T(8,128)(2,1)} custom-call(bf16[256,2048]{1,0:T(8,128)(2,1)} %get-tuple-element.34.h_ref, bf16[2,8512,2048]{2,1,0:T(8,128)(2,1)} %bitcast.3.w_ref), custom_call_target="tpu_custom_call" | custom-call | flops 4294967296 | bytes 16777216 | tf_op jit(solution)/shard_map/pallas_call | solution.py:130
  474.2 1.1 pad_maximum_fusion
  475.3 91.7 %all-reduce.7.cloned.1.call-done = bf16[24,4352]{1,0:T(8,128)(2,1)} async-done(((bf16[24,4352]{1,0:T(8,128)(2,1)}), bf16[24,4352]{1,0:T(8,128)(2,1)}) %all-reduce.7.cloned.1.call-update) | async-done | bytes 208912 | tf_op jit(solution)/shard_map/psum | solution.py:358
  567.0 1.0 reshape.129
  568.1 1.1 copy.16
  569.2 13.7 %shard_map.135.rest_0_ = f32[512,2048]{1,0:T(8,128)} custom-call(bf16[32,256,128]{2,1,0:T(8,128)(2,1)} %copy-done.1, bf16[256,4096]{1,0:T(8,128)(2,1)} %shard_map.134.z_ref, f32[1,4096]{1,0:T(1,128)} %copy-done.13, bf16[2,4096,2048]{2,1,0:T(8,128)(2,1)} %w_ref.7, f32[256,2048]{1,0:T(8,128)} %get-tuple-element.53.resid_ref, f32[1,2048]{1,0:T(1,128)} %slice.128.pre_ref), custom_call_target="tpu_custom_call" | custom-call | flops 4294967296 | bytes 16777216 | tf_op jit(solution)/shard_map/pallas_call | solution.py:296
  582.9 13.8 %shard_map.136 = f32[512,2048]{1,0:T(8,128)} custom-call(bf16[32,256,128]{2,1,0:T(8,128)(2,1)} %all-to-all-done.3.y_ref, bf16[256,4096]{1,0:T(8,128)(2,1)} %shard_map.127.z_ref, f32[1,4096]{1,0:T(1,128)} %copy-done.13, bf16[2,4096,2048]{2,1,0:T(8,128)(2,1)} %w_ref.7, f32[256,2048]{1,0:T(8,128)} %get-tuple-element.38.resid_ref, ...), custom_call_target="tpu_custom_call", output_to_operand_aliasing={{}: (6, {})} | custom-call | flops 4294967296 | bytes 16777216 | tf_op jit(solution)/shard_map/pallas_call | solution.py:296
  (104 shorter events, 14.6 us)
Async XLA Ops:
  7.2 2.8 copy-start.25
  7.2 9.0 %copy-start.14 = (f32[2,4352,4]{1,2,0:T(4,128)S(1)}, f32[2,4352,4]{1,2,0:T(4,128)}, u32[]{:S(2)}) copy-start(f32[2,4352,4]{1,2,0:T(4,128)} %param.13) | copy-start | bytes 417796
  7.2 9.7 %copy-start.23 = (f32[2,4352]{1,0:T(2,128)S(1)}, f32[2,4352]{1,0:T(2,128)}, u32[]{:S(2)}) copy-start(f32[2,4352]{1,0:T(2,128)} %param.14) | copy-start | bytes 104452
  7.2 95.3 %all-gather.13.cloned.1.call-start = ((), (), s32[]{:S(2)}) async-start(), calls=%async_computation.12 | async-start | bytes 4325376 | tf_op jit(solution)/shard_map/all_gather | solution.py:365
  10.0 1.3 copy-start
  11.5 10.2 %collective-permute-start.2 = (bf16[32,2048]{1,0:T(8,128)(2,1)S(1)}, bf16[32,2048]{1,0:T(8,128)(2,1)S(1)}, u32[]{:S(2)}, u32[]{:S(2)}) collective-permute-start(bf16[32,2048]{1,0:T(8,128)(2,1)S(1)} %get-tuple-element.74), channel_id=1, source_target_pairs={{0,1},{1,2},{2,3},{3,4},{4,5},{5,6},{6,7},{7,8},{8,9},{9,10},{10,1... | collective-permute-start | bytes 393224 | tf_op jit(solution)/shard_map/ppermute | solution.py:351
  17.5 3.6 copy-start.26
  21.7 0.7 copy-start.15
  39.3 200.8 %all-gather.9.cloned.1.call-start = ((), (), s32[]{:S(2)}) async-start(), calls=%async_computation.10 | async-start | bytes 4325376 | tf_op jit(solution)/shard_map/all_gather | solution.py:365
  39.3 3.9 collective-permute-start
  43.2 0.7 copy-start.17
  60.8 9.2 %copy-start.27 = (f32[2,64]{1,0:T(2,128)S(1)}, f32[2,64]{1,0:T(2,128)}, u32[]{:S(2)}) copy-start(f32[2,64]{1,0:T(2,128)} %param.16) | copy-start | bytes 1540
  60.9 9.2 %copy-start.28 = (f32[2,64]{1,0:T(2,128)S(1)}, f32[2,64]{1,0:T(2,128)}, u32[]{:S(2)}) copy-start(f32[2,64]{1,0:T(2,128)} %param.17) | copy-start | bytes 1540
  60.9 10.4 %copy-start.20 = (bf16[4,8,4352]{2,1,0:T(8,128)(2,1)S(1)}, bf16[4,8,4352]{2,1,0:T(8,128)(2,1)}, u32[]{:S(2)}) copy-start(bf16[4,8,4352]{2,1,0:T(8,128)(2,1)} %get-tuple-element.41) | copy-start | bytes 835588
  60.9 10.5 %copy-start.21 = (bf16[4,8,4352]{2,1,0:T(8,128)(2,1)S(1)}, bf16[4,8,4352]{2,1,0:T(8,128)(2,1)}, u32[]{:S(2)}) copy-start(bf16[4,8,4352]{2,1,0:T(8,128)(2,1)} %get-tuple-element.42) | copy-start | bytes 835588
  60.9 42.7 %all-to-all-start.4 = ((bf16[32,264,128]{2,1,0:T(8,128)(2,1)}), bf16[32,264,128]{2,1,0:T(8,128)(2,1)S(1)}, u32[]{:S(2)}, u32[]{:S(2)}) async-start(bf16[32,264,128]{2,1,0:T(8,128)(2,1)} %get-tuple-element.39), calls=%async_computation.4 | async-start | bytes 4325376 | tf_op jit(solution)/shard_map/all_to_all | solution.py:364
  103.6 1.3 copy-start.6
  124.4 41.0 %all-to-all-start.5 = ((bf16[32,256,128]{2,1,0:T(8,128)(2,1)}), bf16[32,256,128]{2,1,0:T(8,128)(2,1)S(1)}, u32[]{:S(2)}, u32[]{:S(2)}) async-start(bf16[32,256,128]{2,1,0:T(8,128)(2,1)} %get-tuple-element.44), calls=%async_computation.5 | async-start | bytes 4194304 | tf_op jit(solution)/shard_map/all_to_all | solution.py:376
  128.3 12.4 %copy-start.24 = (f32[2,1,4096]{2,1,0:T(1,128)S(1)}, f32[2,1,4096]{2,1,0:T(1,128)}, u32[]{:S(2)}) copy-start(f32[2,1,4096]{2,1,0:T(1,128)} %param.18) | copy-start | bytes 98308
  128.3 245.1 %all-reduce.5.cloned.1.call-start = ((), (), s32[]{:S(2)}) async-start(), calls=%async_computation.8 | async-start | bytes 417792 | tf_op jit(solution)/shard_map/psum | solution.py:358
  141.3 273.5 %copy-start.13 = (f32[1,4096]{1,0:T(1,128)}, f32[1,4096]{1,0:T(1,128)S(1)}, u32[]{:S(2)}) copy-start(f32[1,4096]{1,0:T(1,128)S(1)} %get-tuple-element.70.gate_ref) | copy-start | bytes 49156
  165.4 1.4 copy-start.2
  182.9 4.5 collective-permute-start.3
  186.1 188.6 %all-gather.15.cloned.1.call-start = ((), (), s32[]{:S(2)}) async-start(), calls=%async_computation.13 | async-start | bytes 4325376 | tf_op jit(solution)/shard_map/all_gather | solution.py:365
  187.4 0.7 copy-start.16
  188.1 17.1 %copy-start.4 = (bf16[32,264,128]{2,1,0:T(8,128)(2,1)S(1)}, bf16[32,264,128]{2,1,0:T(8,128)(2,1)}, u32[]{:S(2)}) copy-start(bf16[32,264,128]{2,1,0:T(8,128)(2,1)} %get-tuple-element.31) | copy-start | bytes 6488068
  259.5 31.8 %all-to-all-start.1 = ((bf16[32,256,128]{2,1,0:T(8,128)(2,1)}), bf16[32,256,128]{2,1,0:T(8,128)(2,1)S(1)}, u32[]{:S(2)}, u32[]{:S(2)}) async-start(bf16[32,256,128]{2,1,0:T(8,128)(2,1)} %get-tuple-element.33), calls=%async_computation.1 | async-start | bytes 4194304 | tf_op jit(solution)/shard_map/all_to_all | solution.py:376
  262.5 152.9 %all-gather.11.cloned.1.call-start = ((), (), s32[]{:S(2)}) async-start(), calls=%async_computation.11 | async-start | bytes 4325376 | tf_op jit(solution)/shard_map/all_gather | solution.py:365
  291.2 1.3 copy-start.3
  308.7 23.4 %copy-start.5 = (bf16[32,264,128]{2,1,0:T(8,128)(2,1)S(1)}, bf16[32,264,128]{2,1,0:T(8,128)(2,1)}, u32[]{:S(2)}) copy-start(bf16[32,264,128]{2,1,0:T(8,128)(2,1)} %get-tuple-element.46) | copy-start | bytes 6488068
  308.7 5.7 collective-permute-start.1
  314.3 0.7 copy-start.18
  370.2 3.3 copy-start.19
  370.2 3.3 copy-start.22
  370.2 39.5 %all-to-all-start.2 = ((bf16[32,264,128]{2,1,0:T(8,128)(2,1)}), bf16[32,264,128]{2,1,0:T(8,128)(2,1)S(1)}, u32[]{:S(2)}, u32[]{:S(2)}) async-start(bf16[32,264,128]{2,1,0:T(8,128)(2,1)} %get-tuple-element.35), calls=%async_computation.2 | async-start | bytes 4325376 | tf_op jit(solution)/shard_map/all_to_all | solution.py:364
  409.7 1.3 copy-start.7
  409.7 5.6 copy-start.8
  409.7 5.6 copy-start.9
  411.1 32.5 %all-to-all-start.7 = ((bf16[32,256,128]{2,1,0:T(8,128)(2,1)}), bf16[32,256,128]{2,1,0:T(8,128)(2,1)S(1)}, u32[]{:S(2)}, u32[]{:S(2)}) async-start(bf16[32,256,128]{2,1,0:T(8,128)(2,1)} %get-tuple-element.52), calls=%async_computation.7 | async-start | bytes 4194304 | tf_op jit(solution)/shard_map/all_to_all | solution.py:376
  443.6 1.4 copy-start.1
  445.0 137.9 %all-to-all-start.3 = ((bf16[32,256,128]{2,1,0:T(8,128)(2,1)}), bf16[32,256,128]{2,1,0:T(8,128)(2,1)}, u32[]{:S(2)}, u32[]{:S(2)}) async-start(bf16[32,256,128]{2,1,0:T(8,128)(2,1)} %get-tuple-element.37), calls=%async_computation.3 | async-start | bytes 4194304 | tf_op jit(solution)/shard_map/all_to_all | solution.py:376
  450.0 117.0 %all-reduce.7.cloned.1.call-start = ((), (), s32[]{:S(2)}) async-start(), calls=%async_computation.9 | async-start | bytes 417792 | tf_op jit(solution)/shard_map/psum | solution.py:358
  462.0 12.0 %copy-start.12 = (bf16[24,4352]{1,0:T(8,128)(2,1)S(1)}, bf16[24,4352]{1,0:T(8,128)(2,1)}, u32[]{:S(2)}) copy-start(bf16[24,4352]{1,0:T(8,128)(2,1)} %all-reduce.5.cloned.1.call-done) | copy-start | bytes 626692
  462.0 12.2 %copy-start.10 = (f32[4,128,128]{2,1,0:T(8,128)S(1)}, f32[4,128,128]{2,1,0:T(8,128)}, u32[]{:S(2)}) copy-start(f32[4,128,128]{2,1,0:T(8,128)} %get-tuple-element.56) | copy-start | bytes 786436
  462.0 12.2 %copy-start.11 = (f32[4,128,128]{2,1,0:T(8,128)S(1)}, f32[4,128,128]{2,1,0:T(8,128)}, u32[]{:S(2)}) copy-start(f32[4,128,128]{2,1,0:T(8,128)} %get-tuple-element.57) | copy-start | bytes 786436
Sparse Core Ops, SparseCore 0:
  39.4 63.0 all-gather.12
  104.6 58.9 all-gather.8
  186.2 110.2 all-reduce.4
  298.5 39.3 all-gather.14
  339.8 68.3 all-gather.10
  474.3 92.6 all-reduce.6

commit v2 on v1

v2 whole, which is shorter than its diff:
```python
import functools

import jax
import jax.numpy as jnp
from jax import lax
from jax.experimental import pallas as pl
from jax.experimental.pallas import tpu as pltpu
from jax.sharding import PartitionSpec as P


CONV_WIDTH = 4
EPSILON = 1e-5
PROMPT_GROUPS = 2
HALO = 8
PACK = 16
LANES = 128
SCAN_UNROLL = 2
NT = (((1,), (1,)), ((), ()))
X_TILE = 512
Z_TILE = 512
OUT_TILE = 512


def silu(values):
    return values * (1.0 / (1.0 + jnp.exp(-values)))


def pick_tile(preferred, total):
    tile = preferred
    while total % tile:
        tile //= 2
    return tile


def start_weights(w_ref, layer, first, tile, buffer, arrived):
    for index in range(buffer.shape[0]):
        pltpu.make_async_copy(w_ref.at[layer, pl.ds(first + index * tile, tile)], buffer.at[index], arrived.at[index]).start()


def wait_weights(w_ref, layer, first, tile, buffer, arrived, index):
    at = pl.ds(pl.multiple_of(first + index * tile, LANES), tile)
    pltpu.make_async_copy(w_ref.at[layer, at], buffer.at[index], arrived.at[index]).wait()


def fill_window(projected, window, n_prompts, seg_len):
    rows = n_prompts * seg_len
    width = window.shape[-1]
    window[:, HALO:, :] = projected[:rows].reshape(n_prompts, seg_len, width)
    window[:, :HALO, :] = projected[rows:].reshape(n_prompts, HALO, width)


def convolve(window, cw_ref, cb_ref, prompt, seg_len, lane_start, col_start):
    acc = cb_ref[:, pl.ds(col_start, LANES)]
    for tap in range(CONV_WIDTH):
        first = HALO - (CONV_WIDTH - 1) + tap
        acc = acc + window[prompt, first:first + seg_len, lane_start:lane_start + LANES] * cw_ref[tap:tap + 1, pl.ds(col_start, LANES)]
    return silu(acc).astype(jnp.bfloat16)


def rounded_product(left, right_rows):
    return lax.dot_general(left, right_rows, NT, preferred_element_type=jnp.float32).astype(jnp.bfloat16).astype(jnp.float32)


def bc_kernel(layer, n_prompts, seg_len, d_inner, d_bc, n_heads, h_ref, halo_ref, w_ref, cw_ref, cb_ref, dtb_ref,
              bc_ref, dt_ref, weights, arrived, h_ext, window, turned, dt_rows, last_rows):
    rows = n_prompts * seg_len
    pair = LANES // seg_len
    dests = n_heads // pair
    first = 2 * d_inner
    start_weights(w_ref, layer, first, d_bc + n_heads, weights, arrived)
    h_ext[:rows] = h_ref[...]
    h_ext[rows:] = halo_ref[...]
    dt_rows[...] = jnp.zeros_like(dt_rows)
    wait_weights(w_ref, layer, first, d_bc + n_heads, weights, arrived, 0)
    fill_window(rounded_product(h_ext[...], weights[0]), window, n_prompts, seg_len)
    per = CONV_WIDTH
    for prompt in range(n_prompts):
        at = slice(prompt * seg_len, (prompt + 1) * seg_len)
        last_rows[prompt * per:(prompt + 1) * per, :] = window[prompt, HALO + seg_len - per:, :d_bc]
        for start in range(0, d_bc, LANES):
            bc_ref[at, start:start + LANES] = convolve(window, cw_ref, cb_ref, prompt, seg_len, start, d_inner + start)
        raw = window[prompt, HALO:, d_bc:d_bc + n_heads] + dtb_ref[:, :n_heads]
        delta = jnp.maximum(raw, 0.0) + jnp.log1p(jnp.exp(-jnp.abs(raw)))
        delta = delta.astype(jnp.bfloat16).astype(jnp.float32)
        turned[...] = jnp.transpose(delta, (1, 0))
        parts = [turned[pl.ds(which, dests, stride=pair), :] for which in range(pair)]
        dt_rows[pl.ds(prompt, dests, stride=PACK), :] = jnp.concatenate(parts, axis=1)
    bc_ref[rows:, :] = last_rows[...].astype(jnp.bfloat16)
    dt_ref[...] = dt_rows[...].astype(jnp.bfloat16)


def project_bc(layer, h, halo, w_rows, conv_w, conv_b, dt_bias, n_prompts, seg_len, d_inner, d_bc):
    rows, d_model = h.shape
    n_heads = dt_bias.shape[-1]
    dests = d_inner // LANES
    m_rows = rows + halo.shape[0]
    vmem = pl.BlockSpec(memory_space=pltpu.VMEM)
    return pl.pallas_call(
        functools.partial(bc_kernel, layer, n_prompts, seg_len, d_inner, d_bc, n_heads),
        in_specs=[vmem, vmem, pl.BlockSpec(memory_space=pl.ANY), vmem, vmem, vmem],
        out_specs=[vmem, vmem],
        out_shape=[jax.ShapeDtypeStruct((rows + n_prompts * CONV_WIDTH, d_bc), jnp.bfloat16),
                   jax.ShapeDtypeStruct((dests * PACK, LANES), jnp.bfloat16)],
        scratch_shapes=[pltpu.VMEM((1, d_bc + n_heads, d_model), jnp.bfloat16),
                        pltpu.SemaphoreType.DMA((1,)),
                        pltpu.VMEM((m_rows, d_model), jnp.bfloat16),
                        pltpu.VMEM((n_prompts, seg_len + HALO, d_bc + n_heads), jnp.float32),
                        pltpu.VMEM((n_heads, seg_len), jnp.float32),
                        pltpu.VMEM((dests * PACK, LANES), jnp.float32),
                        pltpu.VMEM((n_prompts * CONV_WIDTH, d_bc), jnp.float32)],
        cost_estimate=pl.CostEstimate(flops=2 * m_rows * d_model * (d_bc + n_heads), bytes_accessed=2 * d_model * (d_bc + n_heads), transcendentals=0),
    )(h, halo, w_rows, conv_w, conv_b, dt_bias)


def x_kernel(layer, n_prompts, seg_len, d_inner, h_ref, halo_ref, dt_ref, w_ref, cw_ref, cb_ref, xs_ref,
             weights, arrived, h_ext, window, last_rows):
    step = pl.program_id(0)
    rows = n_prompts * seg_len
    tile = weights.shape[1]
    per = CONV_WIDTH

    @pl.when(step == 0)
    def _():
        start_weights(w_ref, layer, d_inner, tile, weights, arrived)
        h_ext[:rows] = h_ref[...]
        h_ext[rows:] = halo_ref[...]

    wait_weights(w_ref, layer, d_inner, tile, weights, arrived, step)
    fill_window(rounded_product(h_ext[...], weights[step]), window, n_prompts, seg_len)
    base = step * tile
    for prompt in range(n_prompts):
        last_rows[prompt * per:(prompt + 1) * per, :] = window[prompt, HALO + seg_len - per:, :]
    for block in range(tile // LANES):
        start = block * LANES
        for prompt in range(n_prompts):
            at = slice(prompt * seg_len, (prompt + 1) * seg_len)
            xs_ref[block, at, :] = convolve(window, cw_ref, cb_ref, prompt, seg_len, start, pl.multiple_of(base + start, LANES))
        dest = step * (tile // LANES) + block
        xs_ref[block, rows:rows + PACK, :] = dt_ref[pl.ds(pl.multiple_of(dest * PACK, PACK), PACK), :]
        xs_ref[block, rows + PACK:, :] = last_rows[:, start:start + LANES].astype(jnp.bfloat16)


def project_x(layer, h, halo, dt_all, w_rows, conv_w, conv_b, n_prompts, seg_len, d_inner):
    rows, d_model = h.shape
    tile = pick_tile(X_TILE, d_inner)
    steps = d_inner // tile
    per = tile // LANES
    m_rows = rows + halo.shape[0]
    sent_rows = rows + PACK + n_prompts * CONV_WIDTH
    whole = lambda *shape: pl.BlockSpec(shape, lambda s: (0,) * len(shape), pipeline_mode=pl.Buffered(1))
    return pl.pallas_call(
        functools.partial(x_kernel, layer, n_prompts, seg_len, d_inner),
        grid=(steps,),
        in_specs=[whole(*h.shape), whole(*halo.shape), whole(*dt_all.shape), pl.BlockSpec(memory_space=pl.ANY),
                  whole(*conv_w.shape), whole(*conv_b.shape)],
        out_specs=pl.BlockSpec((per, sent_rows, LANES), lambda s: (s, 0, 0)),
        out_shape=jax.ShapeDtypeStruct((d_inner // LANES, sent_rows, LANES), jnp.bfloat16),
        scratch_shapes=[pltpu.VMEM((steps, tile, d_model), jnp.bfloat16),
                        pltpu.SemaphoreType.DMA((steps,)),
                        pltpu.VMEM((m_rows, d_model), jnp.bfloat16),
                        pltpu.VMEM((n_prompts, seg_len + HALO, tile), jnp.float32),
                        pltpu.VMEM((n_prompts * CONV_WIDTH, tile), jnp.float32)],
        cost_estimate=pl.CostEstimate(flops=2 * m_rows * d_model * d_inner, bytes_accessed=2 * d_model * d_inner, transcendentals=0),
    )(h, halo, dt_all, w_rows, conv_w, conv_b)


def z_kernel(layer, h_ref, w_ref, z_ref, weights, arrived):
    step = pl.program_id(0)
    tile = weights.shape[1]

    @pl.when(step == 0)
    def _():
        start_weights(w_ref, layer, 0, tile, weights, arrived)

    wait_weights(w_ref, layer, 0, tile, weights, arrived, step)
    z_ref[...] = lax.dot_general(h_ref[...], weights[step], NT, preferred_element_type=jnp.float32).astype(jnp.bfloat16)


def project_z(layer, h, w_rows, d_inner):
    rows, d_model = h.shape
    tile = pick_tile(Z_TILE, d_inner)
    steps = d_inner // tile
    return pl.pallas_call(
        functools.partial(z_kernel, layer),
        grid=(steps,),
        in_specs=[pl.BlockSpec((rows, d_model), lambda s: (0, 0), pipeline_mode=pl.Buffered(1)),
                  pl.BlockSpec(memory_space=pl.ANY)],
        out_specs=pl.BlockSpec((rows, tile), lambda s: (0, s)),
        out_shape=jax.ShapeDtypeStruct((rows, d_inner), jnp.bfloat16),
        scratch_shapes=[pltpu.VMEM((steps, tile, d_model), jnp.bfloat16), pltpu.SemaphoreType.DMA((steps,))],
        cost_estimate=pl.CostEstimate(flops=2 * rows * d_model * d_inner, bytes_accessed=2 * d_model * d_inner, transcendentals=0),
    )(h, w_rows)


def scan_kernel(n_prompts, seg_len, segs, head_dim, d_state, x_ref, last_ref, bc_ref, a_ref, d_ref, y_ref, state_ref,
                row_refs, col_ref, dtc_ref):
    chunk = segs * seg_len
    rows = n_prompts * seg_len
    heads = LANES // head_dim

    @pl.when(pl.program_id(0) == 0)
    def _():
        state_ref[...] = jnp.zeros_like(state_ref)

    token_r = lax.broadcasted_iota(jnp.int32, (chunk, chunk), 0)
    token_c = lax.broadcasted_iota(jnp.int32, (chunk, chunk), 1)
    causal = token_r >= token_c
    lower = causal.astype(jnp.float32)
    upper = (token_r <= token_c).astype(jnp.float32)
    eye = (token_r == token_c).astype(jnp.float32)
    nt = (((1,), (1,)), ((), ()))
    tn = (((0,), (0,)), ((), ()))

    per_seg = [x_ref[seg, rows:rows + PACK, :].astype(jnp.float32)[:HALO] for seg in range(segs)]
    steps = jnp.concatenate([jnp.concatenate([part[:, head * seg_len:(head + 1) * seg_len] for part in per_seg], axis=1)
                             for head in range(heads)], axis=0)
    row_refs[...] = jnp.dot(steps, upper, preferred_element_type=jnp.float32)
    col_ref[...] = lax.dot_general(lower, steps, nt, preferred_element_type=jnp.float32)
    dtc_ref[...] = lax.dot_general(eye, steps, nt, preferred_element_type=jnp.float32)

    lane = lax.broadcasted_iota(jnp.int32, (chunk, LANES), 1)
    state_row = lax.broadcasted_iota(jnp.int32, (LANES, d_state), 0)
    pick = lax.broadcasted_iota(jnp.int32, (chunk, heads * HALO), 1)

    y_ref[:, rows:, :] = jnp.broadcast_to(last_ref[...], (segs,) + last_ref.shape[1:])

    @pl.loop(0, n_prompts, unroll=SCAN_UNROLL)
    def _(prompt):
        at = pl.ds(pl.multiple_of(prompt * seg_len, seg_len), seg_len)
        x_float = x_ref[:, at, :].reshape(chunk, LANES).astype(jnp.float32)
        b_part = bc_ref[:, 0, at, :d_state].reshape(chunk, d_state)
        c_part = bc_ref[:, 0, at, d_state:].reshape(chunk, d_state)
        scores = lax.dot_general(c_part, b_part, nt, preferred_element_type=jnp.float32)
        state = state_ref[prompt]
        y_inter = lax.dot_general(c_part.astype(jnp.float32), state, nt, preferred_element_type=jnp.float32)

        cums = [jnp.sum(jnp.where(pick == head * HALO + prompt, col_ref[...], 0.0), axis=1, keepdims=True) for head in range(heads)]
        dts = [jnp.sum(jnp.where(pick == head * HALO + prompt, dtc_ref[...], 0.0), axis=1, keepdims=True) for head in range(heads)]
        cum_log = jnp.broadcast_to(cums[0] * a_ref[0], (chunk, LANES))
        delta = jnp.broadcast_to(dts[0], (chunk, LANES))
        for head in range(1, heads):
            cum_log = jnp.where(lane >= head * head_dim, cums[head] * a_ref[head], cum_log)
            delta = jnp.where(lane >= head * head_dim, dts[head], delta)
        x_scaled = x_float * delta
        skip = jnp.broadcast_to(d_ref[0], (chunk, LANES))
        for head in range(1, heads):
            skip = jnp.where(lane >= head * head_dim, d_ref[head], skip)

        y_value = y_inter * jnp.exp(cum_log) + skip * x_float
        kept = jnp.zeros((LANES, d_state), jnp.float32)
        for head in range(heads):
            row = row_refs[pl.ds(head * HALO + prompt, 1), :]
            decay = jnp.exp(jnp.where(causal, (cums[head] - row) * a_ref[head], -jnp.inf))
            mine = (lane >= head * head_dim) & (lane < (head + 1) * head_dim)
            y_value = y_value + jnp.dot(decay * scores, jnp.where(mine, x_scaled, 0.0), preferred_element_type=jnp.float32)
            last = jnp.exp(cums[head][chunk - 1:chunk] * a_ref[head])
            kept = jnp.where(state_row >= head * head_dim, last, kept)
        x_left = x_scaled * jnp.exp(cum_log[chunk - 1:chunk] - cum_log)
        state_ref[prompt] = state * kept + lax.dot_general(x_left, b_part.astype(jnp.float32), tn, preferred_element_type=jnp.float32)
        y_ref[:, at, :] = y_value.astype(jnp.bfloat16).reshape(segs, seg_len, LANES)


def scan_heads(group, x_recv, bc_all, a_neg, d_vec, n_prompts, seg_len, head_dim, d_state):
    seg_count, rows_x, _ = x_recv.shape
    rows = n_prompts * seg_len
    heads = LANES // head_dim
    segs = 4
    while seg_count % segs:
        segs //= 2
    chunk = segs * seg_len
    steps = seg_count // segs
    n_last = n_prompts * CONV_WIDTH
    flops = steps * n_prompts * 2 * chunk * LANES * (chunk * (1 + heads) + 2 * d_state)
    return pl.pallas_call(
        functools.partial(scan_kernel, n_prompts, seg_len, segs, head_dim, d_state),
        grid=(steps,),
        in_specs=[pl.BlockSpec((segs, rows_x, LANES), lambda s: (s, 0, 0)),
                  pl.BlockSpec((1, n_last, LANES), lambda s: (seg_count - 1, rows_x // n_last - 1, 0)),
                  pl.BlockSpec((segs, 1, bc_all.shape[2], 2 * d_state), lambda s: (s, group, 0, 0)),
                  pl.BlockSpec(memory_space=pltpu.SMEM),
                  pl.BlockSpec(memory_space=pltpu.SMEM)],
        out_specs=[pl.BlockSpec((segs, rows + n_last, LANES), lambda s: (s, 0, 0)),
                   pl.BlockSpec((n_prompts, LANES, d_state), lambda s: (0, 0, 0))],
        out_shape=[jax.ShapeDtypeStruct((seg_count, rows + n_last, LANES), jnp.bfloat16),
                   jax.ShapeDtypeStruct((n_prompts, LANES, d_state), jnp.float32)],
        scratch_shapes=[pltpu.VMEM((heads * HALO, chunk), jnp.float32),
                        pltpu.VMEM((chunk, heads * HALO), jnp.float32),
                        pltpu.VMEM((chunk, heads * HALO), jnp.float32)],
        cost_estimate=pl.CostEstimate(flops=flops * 4, bytes_accessed=seg_count * rows * 2 * (2 * LANES + 2 * d_state), transcendentals=0),
    )(x_recv, x_recv, bc_all, a_neg, d_vec)


def out_kernel(layer, with_next, n_tiles, y_ref, z_ref, gate_ref, w_ref, resid_ref, pre_ref, *rest):
    if with_next:
        out_ref, h_ref, weights, arrived, normed, gated, kept = rest
    else:
        out_ref, weights, arrived, normed, gated = rest[-5:]
    step = pl.program_id(0)
    blocks = y_ref.shape[0]
    rows = z_ref.shape[0]
    part = gated.shape[0]
    tile = out_ref.shape[-1]

    def fetch(index):
        at = pl.ds(pl.multiple_of(index * tile, tile), tile)
        return pltpu.make_async_copy(w_ref.at[layer, :, at], weights.at[index], arrived.at[index])

    @pl.when(step == 0)
    def _():
        for index in range(n_tiles):
            fetch(index).start()

        @pl.loop(0, rows // part)
        def _(index):
            at = pl.ds(pl.multiple_of(index * part, part), part)
            total = jnp.zeros((part, LANES), jnp.float32)
            for block in range(blocks):
                lanes = slice(block * LANES, (block + 1) * LANES)
                value = y_ref[block, at, :].astype(jnp.float32) * silu(z_ref[at, lanes].astype(jnp.float32))
                total = total + value * value
                gated[:, lanes] = value
            mean_sq = jnp.sum(total, axis=1, keepdims=True) * (1.0 / (blocks * LANES))
            scale = lax.rsqrt(mean_sq + EPSILON)
            for block in range(blocks):
                lanes = slice(block * LANES, (block + 1) * LANES)
                normed[at, lanes] = (gated[:, lanes] * scale * gate_ref[:, lanes]).astype(jnp.bfloat16)

    fetch(step).wait()
    value = resid_ref[...] + jnp.dot(normed[...], weights[step], preferred_element_type=jnp.float32)
    out_ref[...] = value
    if with_next:
        kept[:, pl.ds(pl.multiple_of(step * tile, tile), tile)] = value

        @pl.when(step == n_tiles - 1)
        def _():
            @pl.loop(0, rows // part)
            def _(index):
                at = pl.ds(pl.multiple_of(index * part, part), part)
                row = kept[at, :]
                mean_sq = jnp.mean(row * row, axis=1, keepdims=True)
                h_ref[at, :] = (row * lax.rsqrt(mean_sq + EPSILON) * pre_ref[...]).astype(jnp.bfloat16)


def project_out(layer, y_recv, z, gate_w, w_out, resid, resid_block, next_pre, shared=None, out_block=0, out_rows=None):
    blocks, rows_y, _ = y_recv.shape
    rows = z.shape[0]
    d_inner = blocks * LANES
    d_model = resid.shape[-1]
    tile = pick_tile(OUT_TILE, d_model)
    n_tiles = d_model // tile
    with_next = next_pre is not None
    part = min(32, rows)
    whole = lambda *shape: pl.BlockSpec(shape, lambda s: (0,) * len(shape), pipeline_mode=pl.Buffered(1))
    out_specs = [pl.BlockSpec((rows, tile), lambda s: (out_block, s))]
    out_shape = [jax.ShapeDtypeStruct((out_rows or rows, d_model), jnp.float32)]
    scratch = [pltpu.VMEM((n_tiles, d_inner, tile), jnp.bfloat16), pltpu.SemaphoreType.DMA((n_tiles,)),
               pltpu.VMEM((rows, d_inner), jnp.bfloat16), pltpu.VMEM((part, d_inner), jnp.float32)]
    if with_next:
        out_specs.append(pl.BlockSpec((rows, d_model), lambda s: (0, 0)))
        out_shape.append(jax.ShapeDtypeStruct((rows, d_model), jnp.bfloat16))
        scratch.append(pltpu.VMEM((rows, d_model), jnp.float32))
    else:
        next_pre = gate_w[:, :d_model]
    extra = [] if shared is None else [shared]
    result = pl.pallas_call(
        functools.partial(out_kernel, layer, with_next, n_tiles),
        grid=(n_tiles,),
        in_specs=[whole(blocks, rows_y, LANES), whole(rows, d_inner), whole(1, d_inner),
                  pl.BlockSpec(memory_space=pl.ANY),
                  pl.BlockSpec((rows, tile), lambda s: (resid_block, s)), whole(1, d_model)] + [pl.BlockSpec(memory_space=pl.ANY)] * len(extra),
        input_output_aliases={6: 0} if extra else {},
        out_specs=out_specs,
        out_shape=out_shape,
        scratch_shapes=scratch,
        cost_estimate=pl.CostEstimate(flops=2 * rows * d_inner * d_model, bytes_accessed=2 * d_inner * d_model, transcendentals=0),
    )(y_recv, z, gate_w, w_out, resid, next_pre, *extra)
    return (result[0], result[1]) if with_next else (result[0], None)


def solution(mesh):
    seg_count = mesh.shape['sp']

    def step(resid, pre_norm, w_in, conv_w, conv_b, dt_bias, a_log, d_skip, gate_norm, w_out):
        batch, seg_len, d_model = resid.shape
        n_layers, n_groups, group_width = gate_norm.shape
        d_inner = n_groups * group_width
        n_heads = dt_bias.shape[1]
        conv_dim = conv_b.shape[1]
        d_bc = conv_dim - d_inner
        d_state = d_bc // (2 * n_groups)
        head_dim = d_inner // n_heads
        local_heads = n_heads // seg_count
        assert n_groups == 1 and local_heads * head_dim == LANES and seg_len * 2 == LANES
        seg_index = lax.axis_index('sp')
        n_prompts = batch // PROMPT_GROUPS
        rows = n_prompts * seg_len
        taps = jnp.swapaxes(conv_w, 1, 2)
        a_neg = -jnp.exp(lax.dynamic_slice_in_dim(a_log, seg_index * local_heads, local_heads, axis=1))
        d_local = lax.dynamic_slice_in_dim(d_skip, seg_index * local_heads, local_heads, axis=1)
        hops = [(source, source + 1) for source in range(seg_count - 1)]

        w_rows = jnp.swapaxes(w_in, 1, 2)
        whole_resid = resid.reshape(batch * seg_len, d_model)
        streams = []
        for group in range(PROMPT_GROUPS):
            part = whole_resid[group * rows:(group + 1) * rows]
            mean_sq = jnp.mean(part * part, axis=-1, keepdims=True)
            h = (part * lax.rsqrt(mean_sq + EPSILON) * pre_norm[0]).astype(jnp.bfloat16)
            streams.append((whole_resid, group, h))

        def exchange_halo(parts):
            edges = [h.reshape(n_prompts, seg_len, d_model)[:, seg_len - HALO:].reshape(n_prompts * HALO, d_model) for h in parts]
            halo = lax.ppermute(jnp.concatenate(edges, axis=0), 'sp', hops)
            return [halo[index * n_prompts * HALO:(index + 1) * n_prompts * HALO] for index in range(len(parts))]

        def gather(parts):
            return lax.all_gather(jnp.stack(parts, axis=0), 'sp', axis=0)

        groups = range(PROMPT_GROUPS)
        finals = []
        states = []
        for layer in range(n_layers):
            conv_args = (taps[layer], conv_b[layer][None, :])
            h_all = [item[2] for item in streams]
            if layer == 0:
                halos = exchange_halo(h_all)
            else:
                halos = [exchange_halo([h_all[group]])[0] for group in groups]
            bc_parts = []
            for group in groups:
                bc_parts.append(project_bc(layer, h_all[group], halos[group], w_rows, *conv_args, dt_bias[layer][None, :], n_prompts, seg_len, d_inner, d_bc))
            if layer == 0:
                bc_all = gather([item[0] for item in bc_parts])
                gathered = [(bc_all, group) for group in groups]
            else:
                gathered = [(gather([bc_parts[group][0]]), 0) for group in groups]
            arrived = []
            gates = []
            for group in groups:
                x_send = project_x(layer, h_all[group], halos[group], bc_parts[group][1], w_rows, *conv_args, n_prompts, seg_len, d_inner)
                arrived.append(lax.all_to_all(x_send, 'sp', 0, 0, tiled=True))
                gates.append(project_z(layer, h_all[group], w_rows, d_inner))
            next_streams = []
            layer_finals = []
            layer_tails = []
            shared = None
            for group in groups:
                part, block, _ = streams[group]
                bc_all, at = gathered[group]
                y_send, final = scan_heads(at, arrived[group], bc_all, a_neg[layer], d_local[layer], n_prompts, seg_len, head_dim, d_state)
                layer_finals.append(final.reshape(n_prompts, local_heads, head_dim, d_state))
                y_recv = lax.all_to_all(y_send, 'sp', 0, 0, tiled=True)
                x_tail = y_recv[:, rows:].reshape(-1, n_prompts, CONV_WIDTH, LANES)[:, :, 1:]
                x_tail = jnp.transpose(x_tail, (1, 0, 3, 2)).reshape(n_prompts, d_inner, CONV_WIDTH - 1)
                bc_tail = bc_all[seg_count - 1, at, rows:].reshape(n_prompts, CONV_WIDTH, d_bc)[:, 1:]
                layer_tails.append(jnp.concatenate([x_tail, jnp.swapaxes(bc_tail, 1, 2)], axis=1))
                if layer + 1 == n_layers:
                    shared, _ = project_out(layer, y_recv, gates[group], gate_norm[layer], w_out, part, block, None, shared, group, batch * seg_len)
                else:
                    new_part, new_h = project_out(layer, y_recv, gates[group], gate_norm[layer], w_out, part, block, pre_norm[layer + 1][None, :])
                    next_streams.append((new_part, 0, new_h))
            streams = next_streams
            finals.append(jnp.concatenate(layer_finals, axis=0))
            states.append(jnp.concatenate(layer_tails, axis=0))
        return shared.reshape(batch, seg_len, d_model), jnp.stack(finals, axis=1), jnp.stack(states, axis=1)

    return jax.shard_map(step, mesh=mesh, in_specs=(P('dp', 'sp', None), P(), P(), P(), P(), P(), P(), P(), P(), P()), out_specs=(P('dp', 'sp', None), P('dp', None, 'sp', None, None), P('dp', None, None, None)), check_vma=False)
```

time: 606 us -> 525 us (0.87)
  waiting for transfers between devices: 194 us -> 148 us
  blocking collectives: 73 us -> 46.7 us
  Pallas kernels: 251 us -> 235 us
  starting transfers between devices: 41.2 us -> 47.8 us
    psum x2 -> x0, waiting for transfers between devices: 91.7 us -> none  [step(): summed = lax.optimization_barrier(lax.psum(tail, 'sp'))]
    all_to_all x2 -> x3, waiting for transfers between devices: 16.7 us -> 83.6 us  [step(): arrived.append(lax.all_to_all(x_send, 'sp', 0, 0, tiled=True))]
    all_to_all x2 -> x1, blocking collectives: 73 us -> 46.7 us  [step(): arrived.append(lax.all_to_all(x_send, 'sp', 0, 0, tiled=True))]
    all_gather x4 -> x3, waiting for transfers between devices: 30 us -> 3.85 us  [gather(): return lax.all_gather(jnp.stack(parts, axis=0), 'sp', axis=0)]
    pallas_call x4, Pallas kernels: 77.6 us -> 65.9 us  [scan_heads(): pl.pallas_call(functools.partial(scan_kernel, n_prompts, seg_len, segs, h...]
    all_to_all x4, waiting for transfers between devices: 49.5 us -> 56.8 us  [step(): y_recv = lax.all_to_all(y_send, 'sp', 0, 0, tiled=True)]
    all_to_all x2 -> x3, starting transfers between devices: 12.4 us -> 17 us  [step(): arrived.append(lax.all_to_all(x_send, 'sp', 0, 0, tiled=True))]
    pallas_call x12 -> x16, Pallas kernels: 174 us -> 169 us  [the longest x4 59.8 us: project_x(): pl.pallas_call(functools.partial(x_kernel, layer, n_prompts, seg_len, d_i...]
  transfers between devices with their start and end apart: 16 -> 13, of which waited for: 10 -> 10; matrix products, arithmetic and copies ran while one was open for 3% -> 3% of each run, Pallas kernels for 37% -> 32%
where the time goes in v2:
time: 525 us; the launch traced here: 523 us
  Pallas kernels  235 us (45%)
  waiting for transfers between devices  148 us (28%)
  starting transfers between devices  47.8 us (9%)
  blocking collectives  46.7 us (9%)
  local copies, waits for them, and re-layouts  20 us (4%)
  between operations  14.4 us (3%)
  other arithmetic  10.5 us (2%)
    all_to_all x3, waiting for transfers between devices, step(): arrived.append(lax.all_to_all(x_send, 'sp', 0, 0, tiled=True))  83.6 us
    pallas_call x4, Pallas kernels, scan_heads(): pl.pallas_call(functools.partial(scan_kernel, n_prompts, seg_len, segs, h...  65.9 us
    pallas_call x4, Pallas kernels, project_x(): pl.pallas_call(functools.partial(x_kernel, layer, n_prompts, seg_len, d_i...  59.8 us
    all_to_all x4, waiting for transfers between devices, step(): y_recv = lax.all_to_all(y_send, 'sp', 0, 0, tiled=True)  56.8 us
    pallas_call x4, Pallas kernels, project_out(): pl.pallas_call(functools.partial(out_kernel, layer, with_next, n_tiles),...  52.4 us
    all_to_all x1, blocking collectives, step(): arrived.append(lax.all_to_all(x_send, 'sp', 0, 0, tiled=True))  46.7 us
    pallas_call x4, Pallas kernels, project_z(): pl.pallas_call(functools.partial(z_kernel, layer), grid=(steps,), in_spec...  39 us
    all_to_all x4, starting transfers between devices, step(): y_recv = lax.all_to_all(y_send, 'sp', 0, 0, tiled=True)  18.9 us
  transfers between devices with their start and end apart: 13, of which 10 were waited for; matrix products, arithmetic and copies ran while one was open for 3% of the time, Pallas kernels for 32%

profile of v2, /device:TPU:97, one launch (start us, length us, event | category | flops | bytes accessed | tf_op | source)
XLA Modules:
  0.0 522.9 jit_solution(13381337073793069956)
XLA Ops:
  7.3 2.7 multiply_reduce_fusion
  11.5 4.6 collective-permute-start
  17.6 3.6 fusion.1
  22.4 4.5 shard_map.123
  26.9 4.5 shard_map.121
  31.5 1.6 pad_maximum_fusion.2
  33.2 15.0 %shard_map.131 = bf16[32,288,128]{2,1,0:T(8,128)(2,1)} custom-call(bf16[256,2048]{1,0:T(8,128)(2,1)} %get-tuple-element.65.h_ref, bf16[32,2048]{1,0:T(8,128)(2,1)} %get-tuple-element.55.halo_ref, bf16[512,128]{1,0:T(8,128)(2,1)} %get-tuple-element.32.dt_ref, bf16[2,8512,2048]{2,1,0:T(8,128)(2,1)} %bitcast.4.w_ref, f32[4,4352]{1,0:T(4,128)} %get-tuple-element.58.cw_ref, ...), custom_call_target="tpu_custom_call" | custom-call | flops 4831838208 | bytes 16777216 | tf_op jit(solution)/shard_map/pallas_call | solution.py:151
  48.2 7.6 %all-to-all-start.4 = ((bf16[32,288,128]{2,1,0:T(8,128)(2,1)}), bf16[32,288,128]{2,1,0:T(8,128)(2,1)S(1)}, u32[]{:S(2)}, u32[]{:S(2)}) async-start(bf16[32,288,128]{2,1,0:T(8,128)(2,1)} %shard_map.131), calls=%async_computation.4 | async-start | bytes 4718592 | tf_op jit(solution)/shard_map/all_to_all | solution.py:441
  57.0 43.8 %all-to-all-done.4.x_ref.last_ref = bf16[32,288,128]{2,1,0:T(8,128)(2,1)S(1)} async-done(((bf16[32,288,128]{2,1,0:T(8,128)(2,1)}), bf16[32,288,128]{2,1,0:T(8,128)(2,1)S(1)}, u32[]{:S(2)}, u32[]{:S(2)}) %all-to-all-start.4) | async-done | bytes 2359328 | tf_op jit(solution)/shard_map/all_to_all | solution.py:441
  100.8 3.8 all-gather.7.cloned.1.call-done
  104.6 16.5 %shard_map.132 = (bf16[32,272,128]{2,1,0:T(8,128)(2,1)}, f32[4,128,128]{2,1,0:T(8,128)}) custom-call(bf16[32,288,128]{2,1,0:T(8,128)(2,1)} %copy-done.4, bf16[32,288,128]{2,1,0:T(8,128)(2,1)} %copy-done.4, bf16[32,2,272,256]{3,2,1,0:T(8,128)(2,1)} %bitcast.138, f32[2]{0:T(128)} %get-tuple-element.72.a_ref, f32[2]{0:T(128)} %get-tuple-element.70.d_ref), custom_call_target="tpu_custom_call" | custom-call | flops 8589934592 | bytes 8388608 | tf_op jit(solution)/shard_map/pallas_call | solution.py:274
  121.1 4.6 all-to-all-start.5
  125.8 9.7 %shard_map.133.z_ref = bf16[256,4096]{1,0:T(8,128)(2,1)} custom-call(bf16[256,2048]{1,0:T(8,128)(2,1)} %get-tuple-element.65.h_ref, bf16[2,8512,2048]{2,1,0:T(8,128)(2,1)} %bitcast.4.w_ref), custom_call_target="tpu_custom_call" | custom-call | flops 4294967296 | bytes 16777216 | tf_op jit(solution)/shard_map/pallas_call | solution.py:183
  136.1 19.0 %all-to-all-done.5.y_ref = bf16[32,272,128]{2,1,0:T(8,128)(2,1)S(1)} async-done(((bf16[32,272,128]{2,1,0:T(8,128)(2,1)}), bf16[32,272,128]{2,1,0:T(8,128)(2,1)S(1)}, u32[]{:S(2)}, u32[]{:S(2)}) %all-to-all-start.5) | async-done | bytes 2228256 | tf_op jit(solution)/shard_map/all_to_all | solution.py:452
  155.1 1.4 copy-done.2
  156.5 13.9 %shard_map.134 = (f32[256,2048]{1,0:T(8,128)}, bf16[256,2048]{1,0:T(8,128)(2,1)}) custom-call(bf16[32,272,128]{2,1,0:T(8,128)(2,1)} %copy-done.2, bf16[256,4096]{1,0:T(8,128)(2,1)} %shard_map.133.z_ref, f32[1,4096]{1,0:T(1,128)} %get-tuple-element.62.gate_ref, bf16[2,4096,2048]{2,1,0:T(8,128)(2,1)} %w_ref.7, f32[512,2048]{1,0:T(8,128)} %bitcast.112, ...), custom_call_target="tpu_custom_call" | custom-call | flops 4294967296 | bytes 16777216 | tf_op jit(solution)/shard_map/pallas_call | solution.py:365
  171.3 3.5 collective-permute-start.2
  174.8 1.9 collective-permute-done.2.halo_ref
  177.4 4.5 shard_map.135
  181.9 15.0 %shard_map.122 = bf16[32,288,128]{2,1,0:T(8,128)(2,1)} custom-call(bf16[256,2048]{1,0:T(8,128)(2,1)} %get-tuple-element.66.h_ref, bf16[32,2048]{1,0:T(8,128)(2,1)} %get-tuple-element.56.halo_ref, bf16[512,128]{1,0:T(8,128)(2,1)} %get-tuple-element.23.dt_ref, bf16[2,8512,2048]{2,1,0:T(8,128)(2,1)} %bitcast.4.w_ref, f32[4,4352]{1,0:T(4,128)} %get-tuple-element.58.cw_ref, ...), custom_call_target="tpu_custom_call" | custom-call | flops 4831838208 | bytes 16777216 | tf_op jit(solution)/shard_map/pallas_call | solution.py:151
  196.9 46.7 %all_to_all.40.x_ref.last_ref = bf16[32,288,128]{2,1,0:T(8,128)(2,1)} all-to-all(bf16[32,288,128]{2,1,0:T(8,128)(2,1)} %shard_map.122), channel_id=1, replica_groups=mesh['dp'=1,'sp'=32] {'sp'}, dimensions={0} | all-to-all | bytes 4718592 | tf_op jit(solution)/shard_map/all_to_all | solution.py:441
  243.6 16.5 %shard_map.124 = (bf16[32,272,128]{2,1,0:T(8,128)(2,1)}, f32[4,128,128]{2,1,0:T(8,128)}) custom-call(bf16[32,288,128]{2,1,0:T(8,128)(2,1)} %all_to_all.40.x_ref.last_ref, bf16[32,288,128]{2,1,0:T(8,128)(2,1)} %all_to_all.40.x_ref.last_ref, bf16[32,2,272,256]{3,2,1,0:T(8,128)(2,1)} %bitcast.139, f32[2]{0:T(128)} %get-tuple-element.72.a_ref, ...), custom_call_target="tpu_custom_call" | custom-call | flops 8589934592 | bytes 8388608 | tf_op jit(solution)/shard_map/pallas_call | solution.py:274
  260.1 3.1 all-to-all-start.1
  263.2 9.7 %shard_map.125.z_ref = bf16[256,4096]{1,0:T(8,128)(2,1)} custom-call(bf16[256,2048]{1,0:T(8,128)(2,1)} %get-tuple-element.66.h_ref, bf16[2,8512,2048]{2,1,0:T(8,128)(2,1)} %bitcast.4.w_ref), custom_call_target="tpu_custom_call" | custom-call | flops 4294967296 | bytes 16777216 | tf_op jit(solution)/shard_map/pallas_call | solution.py:183
  273.0 19.8 %all-to-all-done.1.y_ref = bf16[32,272,128]{2,1,0:T(8,128)(2,1)S(1)} async-done(((bf16[32,272,128]{2,1,0:T(8,128)(2,1)}), bf16[32,272,128]{2,1,0:T(8,128)(2,1)S(1)}, u32[]{:S(2)}, u32[]{:S(2)}) %all-to-all-start.1) | async-done | bytes 2228256 | tf_op jit(solution)/shard_map/all_to_all | solution.py:452
  292.8 1.4 copy-done.3
  294.2 13.8 %shard_map.126 = (f32[256,2048]{1,0:T(8,128)}, bf16[256,2048]{1,0:T(8,128)(2,1)}) custom-call(bf16[32,272,128]{2,1,0:T(8,128)(2,1)} %copy-done.3, bf16[256,4096]{1,0:T(8,128)(2,1)} %shard_map.125.z_ref, f32[1,4096]{1,0:T(1,128)} %get-tuple-element.62.gate_ref, bf16[2,4096,2048]{2,1,0:T(8,128)(2,1)} %w_ref.7, f32[512,2048]{1,0:T(8,128)} %bitcast.113, ...), custom_call_target="tpu_custom_call" | custom-call | flops 4294967296 | bytes 16777216 | tf_op jit(solution)/shard_map/pallas_call | solution.py:365
  308.9 3.6 collective-permute-start.1
  312.5 1.9 collective-permute-done.1.halo_ref
  315.1 4.5 shard_map.127
  319.7 15.0 %shard_map.136 = bf16[32,288,128]{2,1,0:T(8,128)(2,1)} custom-call(bf16[256,2048]{1,0:T(8,128)(2,1)} %get-tuple-element.34.h_ref, bf16[32,2048]{1,0:T(8,128)(2,1)} %copy-done.7, bf16[512,128]{1,0:T(8,128)(2,1)} %get-tuple-element.35.dt_ref, bf16[2,8512,2048]{2,1,0:T(8,128)(2,1)} %bitcast.4.w_ref, f32[4,4352]{1,0:T(4,128)} %get-tuple-element.57.cw_ref, ...), custom_call_target="tpu_custom_call" | custom-call | flops 4831838208 | bytes 16777216 | tf_op jit(solution)/shard_map/pallas_call | solution.py:151
  334.6 6.4 %all-to-all-start.6 = ((bf16[32,288,128]{2,1,0:T(8,128)(2,1)}), bf16[32,288,128]{2,1,0:T(8,128)(2,1)S(1)}, u32[]{:S(2)}, u32[]{:S(2)}) async-start(bf16[32,288,128]{2,1,0:T(8,128)(2,1)} %shard_map.136), calls=%async_computation.6 | async-start | bytes 4718592 | tf_op jit(solution)/shard_map/all_to_all | solution.py:441
  341.0 15.0 %shard_map.128 = bf16[32,288,128]{2,1,0:T(8,128)(2,1)} custom-call(bf16[256,2048]{1,0:T(8,128)(2,1)} %get-tuple-element.27.h_ref, bf16[32,2048]{1,0:T(8,128)(2,1)} %copy-done.8, bf16[512,128]{1,0:T(8,128)(2,1)} %get-tuple-element.28.dt_ref, bf16[2,8512,2048]{2,1,0:T(8,128)(2,1)} %bitcast.4.w_ref, f32[4,4352]{1,0:T(4,128)} %get-tuple-element.57.cw_ref, ...), custom_call_target="tpu_custom_call" | custom-call | flops 4831838208 | bytes 16777216 | tf_op jit(solution)/shard_map/pallas_call | solution.py:151
  356.0 25.2 %all-to-all-done.6.x_ref.last_ref = bf16[32,288,128]{2,1,0:T(8,128)(2,1)S(1)} async-done(((bf16[32,288,128]{2,1,0:T(8,128)(2,1)}), bf16[32,288,128]{2,1,0:T(8,128)(2,1)S(1)}, u32[]{:S(2)}, u32[]{:S(2)}) %all-to-all-start.6) | async-done | bytes 2359328 | tf_op jit(solution)/shard_map/all_to_all | solution.py:441
  381.2 1.4 copy-done.6
  382.6 3.1 all-to-all-start.2
  385.7 16.5 %shard_map.137 = (bf16[32,272,128]{2,1,0:T(8,128)(2,1)}, f32[4,128,128]{2,1,0:T(8,128)}) custom-call(bf16[32,288,128]{2,1,0:T(8,128)(2,1)} %copy-done.6, bf16[32,288,128]{2,1,0:T(8,128)(2,1)} %copy-done.6, bf16[32,1,272,256]{3,2,1,0:T(8,128)(2,1)} %bitcast.141, f32[2]{0:T(128)} %get-tuple-element.71.a_ref, f32[2]{0:T(128)} %get-tuple-element.69.d_ref), custom_call_target="tpu_custom_call" | custom-call | flops 8589934592 | bytes 8388608 | tf_op jit(solution)/shard_map/pallas_call | solution.py:274
  402.2 14.6 %all-to-all-done.2.x_ref.last_ref = bf16[32,288,128]{2,1,0:T(8,128)(2,1)S(1)} async-done(((bf16[32,288,128]{2,1,0:T(8,128)(2,1)}), bf16[32,288,128]{2,1,0:T(8,128)(2,1)S(1)}, u32[]{:S(2)}, u32[]{:S(2)}) %all-to-all-start.2) | async-done | bytes 2359328 | tf_op jit(solution)/shard_map/all_to_all | solution.py:441
  416.8 1.4 copy-done.5
  418.2 5.2 all-to-all-start.7
  423.4 16.5 %shard_map.129 = (bf16[32,272,128]{2,1,0:T(8,128)(2,1)}, f32[4,128,128]{2,1,0:T(8,128)}) custom-call(bf16[32,288,128]{2,1,0:T(8,128)(2,1)} %copy-done.5, bf16[32,288,128]{2,1,0:T(8,128)(2,1)} %copy-done.5, bf16[32,1,272,256]{3,2,1,0:T(8,128)(2,1)} %bitcast.143, f32[2]{0:T(128)} %get-tuple-element.71.a_ref, f32[2]{0:T(128)} %get-tuple-element.69.d_ref), custom_call_target="tpu_custom_call" | custom-call | flops 8589934592 | bytes 8388608 | tf_op jit(solution)/shard_map/pallas_call | solution.py:274
  439.9 13.2 %all-to-all-done.7.y_ref = bf16[32,272,128]{2,1,0:T(8,128)(2,1)S(1)} async-done(((bf16[32,272,128]{2,1,0:T(8,128)(2,1)}), bf16[32,272,128]{2,1,0:T(8,128)(2,1)S(1)}, u32[]{:S(2)}, u32[]{:S(2)}) %all-to-all-start.7) | async-done | bytes 2228256 | tf_op jit(solution)/shard_map/all_to_all | solution.py:452
  453.2 6.0 %all-to-all-start.3 = ((bf16[32,272,128]{2,1,0:T(8,128)(2,1)}), bf16[32,272,128]{2,1,0:T(8,128)(2,1)}, u32[]{:S(2)}, u32[]{:S(2)}) async-start(bf16[32,272,128]{2,1,0:T(8,128)(2,1)} %get-tuple-element.30), calls=%async_computation.3 | async-start | bytes 4456448 | tf_op jit(solution)/shard_map/all_to_all | solution.py:452
  461.0 9.7 %shard_map.138.z_ref = bf16[256,4096]{1,0:T(8,128)(2,1)} custom-call(bf16[256,2048]{1,0:T(8,128)(2,1)} %get-tuple-element.34.h_ref, bf16[2,8512,2048]{2,1,0:T(8,128)(2,1)} %bitcast.4.w_ref), custom_call_target="tpu_custom_call" | custom-call | flops 4294967296 | bytes 16777216 | tf_op jit(solution)/shard_map/pallas_call | solution.py:183
  470.8 9.8 %shard_map.130.z_ref = bf16[256,4096]{1,0:T(8,128)(2,1)} custom-call(bf16[256,2048]{1,0:T(8,128)(2,1)} %get-tuple-element.27.h_ref, bf16[2,8512,2048]{2,1,0:T(8,128)(2,1)} %bitcast.4.w_ref), custom_call_target="tpu_custom_call" | custom-call | flops 4294967296 | bytes 16777216 | tf_op jit(solution)/shard_map/pallas_call | solution.py:183
  484.4 4.8 all-to-all-done.3.y_ref
  491.5 12.4 %shard_map.139.rest_0_ = f32[512,2048]{1,0:T(8,128)} custom-call(bf16[32,272,128]{2,1,0:T(8,128)(2,1)} %copy-done.1, bf16[256,4096]{1,0:T(8,128)(2,1)} %shard_map.138.z_ref, f32[1,4096]{1,0:T(1,128)} %get-tuple-element.61.gate_ref, bf16[2,4096,2048]{2,1,0:T(8,128)(2,1)} %w_ref.7, f32[256,2048]{1,0:T(8,128)} %get-tuple-element.38.resid_ref, ...), custom_call_target="tpu_custom_call" | custom-call | flops 4294967296 | bytes 16777216 | tf_op jit(solution)/shard_map/pallas_call | solution.py:365
  503.9 12.4 %shard_map.140 = f32[512,2048]{1,0:T(8,128)} custom-call(bf16[32,272,128]{2,1,0:T(8,128)(2,1)} %all-to-all-done.3.y_ref, bf16[256,4096]{1,0:T(8,128)(2,1)} %shard_map.130.z_ref, f32[1,4096]{1,0:T(1,128)} %get-tuple-element.61.gate_ref, bf16[2,4096,2048]{2,1,0:T(8,128)(2,1)} %w_ref.7, ...), custom_call_target="tpu_custom_call", output_to_operand_aliasing={{}: (6, {})} | custom-call | flops 4294967296 | bytes 16777216 | tf_op jit(solution)/shard_map/pallas_call | solution.py:365
  (106 shorter events, 17.4 us)
Async XLA Ops:
  7.2 3.0 copy-start.17
  7.2 9.1 %copy-start.13 = (f32[2,4352,4]{1,2,0:T(4,128)S(1)}, f32[2,4352,4]{1,2,0:T(4,128)}, u32[]{:S(2)}) copy-start(f32[2,4352,4]{1,2,0:T(4,128)} %param.13) | copy-start | bytes 417796
  7.2 9.7 %copy-start.15 = (f32[2,4352]{1,0:T(2,128)S(1)}, f32[2,4352]{1,0:T(2,128)}, u32[]{:S(2)}) copy-start(f32[2,4352]{1,0:T(2,128)} %param.14) | copy-start | bytes 104452
  7.2 97.4 %all-gather.7.cloned.1.call-start = ((), (), s32[]{:S(2)}) async-start(), calls=%async_computation.8 | async-start | bytes 9191424 | tf_op jit(solution)/shard_map/all_gather | solution.py:417
  10.0 1.3 copy-start
  11.5 10.2 %collective-permute-start = (bf16[64,2048]{1,0:T(8,128)(2,1)S(1)}, bf16[64,2048]{1,0:T(8,128)(2,1)S(1)}, u32[]{:S(2)}, u32[]{:S(2)}) collective-permute-start(bf16[64,2048]{1,0:T(8,128)(2,1)S(1)} %pad_maximum_fusion.3), channel_id=1, source_target_pairs={{0,1},{1,2},{2,3},{3,4},{4,5},{5,6},{6,7},{7,8},{8,9},{9,10},{10,1... | collective-permute-start | bytes 786440 | tf_op jit(solution)/shard_map/ppermute | solution.py:413
  17.6 3.6 copy-start.18
  26.9 4.5 copy-start.14
  48.1 7.6 %copy-start.19 = (f32[2,64]{1,0:T(2,128)S(1)}, f32[2,64]{1,0:T(2,128)}, u32[]{:S(2)}) copy-start(f32[2,64]{1,0:T(2,128)} %param.16) | copy-start | bytes 1540
  48.1 7.6 %copy-start.20 = (f32[2,64]{1,0:T(2,128)S(1)}, f32[2,64]{1,0:T(2,128)}, u32[]{:S(2)}) copy-start(f32[2,64]{1,0:T(2,128)} %param.17) | copy-start | bytes 1540
  48.2 52.7 %all-to-all-start.4 = ((bf16[32,288,128]{2,1,0:T(8,128)(2,1)}), bf16[32,288,128]{2,1,0:T(8,128)(2,1)S(1)}, u32[]{:S(2)}, u32[]{:S(2)}) async-start(bf16[32,288,128]{2,1,0:T(8,128)(2,1)} %shard_map.131), calls=%async_computation.4 | async-start | bytes 4718592 | tf_op jit(solution)/shard_map/all_to_all | solution.py:441
  100.8 3.8 copy-start.4
  121.1 34.0 %all-to-all-start.5 = ((bf16[32,272,128]{2,1,0:T(8,128)(2,1)}), bf16[32,272,128]{2,1,0:T(8,128)(2,1)S(1)}, u32[]{:S(2)}, u32[]{:S(2)}) async-start(bf16[32,272,128]{2,1,0:T(8,128)(2,1)} %get-tuple-element.33), calls=%async_computation.5 | async-start | bytes 4456448 | tf_op jit(solution)/shard_map/all_to_all | solution.py:452
  125.7 9.8 %copy-start.16 = (f32[2,1,4096]{2,1,0:T(1,128)S(1)}, f32[2,1,4096]{2,1,0:T(1,128)}, u32[]{:S(2)}) copy-start(f32[2,1,4096]{2,1,0:T(1,128)} %param.18) | copy-start | bytes 98308
  125.7 260.0 %all-gather.11.cloned.1.call-start = ((), (), s32[]{:S(2)}) async-start(), calls=%async_computation.10 | async-start | bytes 4595712 | tf_op jit(solution)/shard_map/all_gather | solution.py:417
  155.1 1.4 copy-start.2
  171.3 5.5 %collective-permute-start.2 = (bf16[32,2048]{1,0:T(8,128)(2,1)S(1)}, bf16[32,2048]{1,0:T(8,128)(2,1)S(1)}, u32[]{:S(2)}, u32[]{:S(2)}) collective-permute-start(bf16[32,2048]{1,0:T(8,128)(2,1)S(1)} %slice_bitcast_fusion), channel_id=1, source_target_pairs={{0,1},{1,2},{2,3},{3,4},{4,5},{5,6},{6,7},{7,8},{8,9},{9,10},{10,1... | collective-permute-start | bytes 393224 | tf_op jit(solution)/shard_map/ppermute | solution.py:413
  176.8 0.7 copy-start.7
  260.1 32.7 %all-to-all-start.1 = ((bf16[32,272,128]{2,1,0:T(8,128)(2,1)}), bf16[32,272,128]{2,1,0:T(8,128)(2,1)S(1)}, u32[]{:S(2)}, u32[]{:S(2)}) async-start(bf16[32,272,128]{2,1,0:T(8,128)(2,1)} %get-tuple-element.26), calls=%async_computation.1 | async-start | bytes 4456448 | tf_op jit(solution)/shard_map/all_to_all | solution.py:452
  263.1 160.3 %all-gather.9.cloned.1.call-start = ((), (), s32[]{:S(2)}) async-start(), calls=%async_computation.9 | async-start | bytes 4595712 | tf_op jit(solution)/shard_map/all_gather | solution.py:417
  292.8 1.4 copy-start.3
  308.9 5.6 %collective-permute-start.1 = (bf16[32,2048]{1,0:T(8,128)(2,1)S(1)}, bf16[32,2048]{1,0:T(8,128)(2,1)S(1)}, u32[]{:S(2)}, u32[]{:S(2)}) collective-permute-start(bf16[32,2048]{1,0:T(8,128)(2,1)S(1)} %slice_bitcast_fusion.1), channel_id=1, source_target_pairs={{0,1},{1,2},{2,3},{3,4},{4,5},{5,6},{6,7},{7,8},{8,9},{9,10},{10,1... | collective-permute-start | bytes 393224 | tf_op jit(solution)/shard_map/ppermute | solution.py:413
  314.4 0.7 copy-start.8
  334.6 46.5 %all-to-all-start.6 = ((bf16[32,288,128]{2,1,0:T(8,128)(2,1)}), bf16[32,288,128]{2,1,0:T(8,128)(2,1)S(1)}, u32[]{:S(2)}, u32[]{:S(2)}) async-start(bf16[32,288,128]{2,1,0:T(8,128)(2,1)} %shard_map.136), calls=%async_computation.6 | async-start | bytes 4718592 | tf_op jit(solution)/shard_map/all_to_all | solution.py:441
  381.2 1.4 copy-start.6
  382.6 34.2 %all-to-all-start.2 = ((bf16[32,288,128]{2,1,0:T(8,128)(2,1)}), bf16[32,288,128]{2,1,0:T(8,128)(2,1)S(1)}, u32[]{:S(2)}, u32[]{:S(2)}) async-start(bf16[32,288,128]{2,1,0:T(8,128)(2,1)} %shard_map.128), calls=%async_computation.2 | async-start | bytes 4718592 | tf_op jit(solution)/shard_map/all_to_all | solution.py:441
  416.8 1.4 copy-start.5
  418.2 34.9 %all-to-all-start.7 = ((bf16[32,272,128]{2,1,0:T(8,128)(2,1)}), bf16[32,272,128]{2,1,0:T(8,128)(2,1)S(1)}, u32[]{:S(2)}, u32[]{:S(2)}) async-start(bf16[32,272,128]{2,1,0:T(8,128)(2,1)} %get-tuple-element.37), calls=%async_computation.7 | async-start | bytes 4456448 | tf_op jit(solution)/shard_map/all_to_all | solution.py:452
  453.1 31.1 %copy-start.1 = (bf16[32,272,128]{2,1,0:T(8,128)(2,1)}, bf16[32,272,128]{2,1,0:T(8,128)(2,1)S(1)}, u32[]{:S(2)}) copy-start(bf16[32,272,128]{2,1,0:T(8,128)(2,1)S(1)} %all-to-all-done.7.y_ref) | copy-start | bytes 6684676
  453.1 6.1 %copy-start.12 = (f32[1,4096]{1,0:T(1,128)S(1)}, f32[1,4096]{1,0:T(1,128)}, u32[]{:S(2)}) copy-start(f32[1,4096]{1,0:T(1,128)} %get-tuple-element.61.gate_ref) | copy-start | bytes 49156
  453.1 7.5 %copy-start.9 = (f32[4,128,128]{2,1,0:T(8,128)S(1)}, f32[4,128,128]{2,1,0:T(8,128)}, u32[]{:S(2)}) copy-start(f32[4,128,128]{2,1,0:T(8,128)} %get-tuple-element.39) | copy-start | bytes 786436
  453.1 7.5 %copy-start.10 = (f32[4,128,128]{2,1,0:T(8,128)S(1)}, f32[4,128,128]{2,1,0:T(8,128)}, u32[]{:S(2)}) copy-start(f32[4,128,128]{2,1,0:T(8,128)} %get-tuple-element.40) | copy-start | bytes 786436
  453.2 7.5 %slice-start = ((bf16[32,272,128]{2,1,0:T(8,128)(2,1)}), bf16[32,16,128]{2,1,0:T(8,128)(2,1)S(1)}, s32[]{:S(2)}) async-start(bf16[32,272,128]{2,1,0:T(8,128)(2,1)} %copy-done.2), calls=%async_computation.11 | async-start | bytes 262144 | tf_op jit(solution)/shard_map/slice | solution.py:453
  453.2 36.0 %all-to-all-start.3 = ((bf16[32,272,128]{2,1,0:T(8,128)(2,1)}), bf16[32,272,128]{2,1,0:T(8,128)(2,1)}, u32[]{:S(2)}, u32[]{:S(2)}) async-start(bf16[32,272,128]{2,1,0:T(8,128)(2,1)} %get-tuple-element.30), calls=%async_computation.3 | async-start | bytes 4456448 | tf_op jit(solution)/shard_map/all_to_all | solution.py:452
  459.2 1.6 slice-start.1
  470.8 11.4 %copy-start.11 = (f32[4,128,128]{2,1,0:T(8,128)S(1)}, f32[4,128,128]{2,1,0:T(8,128)}, u32[]{:S(2)}) copy-start(f32[4,128,128]{2,1,0:T(8,128)} %get-tuple-element.41) | copy-start | bytes 786436
Sparse Core Ops, SparseCore 0:
  33.3 71.3 all-gather.6
  182.1 60.6 all-gather.10
  319.8 61.4 all-gather.8
